TPU v7x, 8 devices: a whole 2x2x1 slice. The times are simulated.
8 devices in a mesh: replica: 1 (over z), heads: 2 (over y), model: 4 (over x, core).
Axes of the slice: x: 2, y: 2, z: 1, core: 2. Of those that a mesh axis runs over, the one named last changes fastest.
Arguments:
- tokens: bfloat16 [128, 18432], P('replica')
- w_query: bfloat16 [18432, 12288], P(None, ('heads', 'model'))
- w_key: bfloat16 [18432, 256], replicated
- w_value: bfloat16 [18432, 256], replicated
- w_out: bfloat16 [12288, 18432], P(('heads', 'model'))
- key_cache: bfloat16 [128, 1, 4096, 256], P(('replica', 'model'))
- value_cache: bfloat16 [128, 1, 4096, 256], P(('replica', 'model'))
- lengths: int32 [128], P(('replica', 'model'))
Outputs:
- output 1: bfloat16 [128, 18432], P('replica')
- output 2: bfloat16 [128, 1, 256], P(('replica', 'model'))
- output 3: bfloat16 [128, 1, 256], P(('replica', 'model'))
All inputs are finite; a program needn't handle non-finite values.
Results may differ from a plain program's by a relative error of at most 0.00214.
Values are sent between devices in bfloat16 or wider.
A program may use at most 1.25 GiB of HBM per device.

v0:
```python
import jax
import jax.numpy as jnp
from jax import lax
from jax.sharding import PartitionSpec as P


def attend(queries, key_rows, value_rows, key_last, value_last, seq_len):
    score_scale = queries.shape[-1] ** -0.5
    scores = jnp.einsum("bgrd,bgtd->bgrt", queries, key_rows, preferred_element_type=jnp.float32) * score_scale
    score_new = jnp.einsum("bgrd,bgd->bgr", queries, key_last, preferred_element_type=jnp.float32) * score_scale
    positions = lax.broadcasted_iota(jnp.int32, (1, 1, 1, key_rows.shape[2]), 3)
    scores = jnp.where(positions < seq_len[:, None, None, None], scores, -jnp.inf)
    score_max = jnp.maximum(jnp.max(scores, axis=-1), score_new)
    weights = jnp.exp(scores - score_max[..., None])
    weight_new = jnp.exp(score_new - score_max)
    denom_sum = jnp.sum(weights, axis=-1) + weight_new
    weighted_sum = jnp.einsum("bgrt,bgtd->bgrd", weights.astype(jnp.bfloat16), value_rows, preferred_element_type=jnp.float32)
    weighted_sum = weighted_sum + weight_new.astype(jnp.bfloat16).astype(jnp.float32)[..., None] * value_last.astype(jnp.float32)[:, :, None, :]
    return (weighted_sum / denom_sum[..., None]).astype(jnp.bfloat16)


def solution(mesh):
    heads_count = mesh.shape["heads"]
    model_count = mesh.shape["model"]

    def local_step(tokens, w_query, w_key, w_value, w_out, key_cache, value_cache, lengths):
        batch_all = tokens.shape[0]
        local_rows = key_cache.shape[0]
        kv_count = key_cache.shape[1]
        head_dim = key_cache.shape[3]
        heads_local = w_query.shape[1] // head_dim
        heads_shard = heads_local * model_count
        group_size = heads_shard * heads_count // kv_count
        shard_groups = max(1, heads_shard // group_size)
        head_index = lax.axis_index("heads")
        model_index = lax.axis_index("model")
        queries = jnp.dot(tokens, w_query, preferred_element_type=jnp.float32).astype(jnp.bfloat16)
        queries = lax.all_to_all(queries.reshape(batch_all, heads_local, head_dim), "model", 0, 1, tiled=True)
        own_tokens = lax.dynamic_slice_in_dim(tokens, model_index * local_rows, local_rows, 0)
        key_new = jnp.dot(own_tokens, w_key, preferred_element_type=jnp.float32).astype(jnp.bfloat16)
        key_new = key_new.reshape(local_rows, kv_count, head_dim)
        value_new = jnp.dot(own_tokens, w_value, preferred_element_type=jnp.float32).astype(jnp.bfloat16)
        value_new = value_new.reshape(local_rows, kv_count, head_dim)
        first_group = head_index * heads_shard // group_size
        attended = attend(
            queries.reshape(local_rows, shard_groups, heads_shard // shard_groups, head_dim),
            lax.dynamic_slice_in_dim(key_cache, first_group, shard_groups, 1),
            lax.dynamic_slice_in_dim(value_cache, first_group, shard_groups, 1),
            lax.dynamic_slice_in_dim(key_new, first_group, shard_groups, 1),
            lax.dynamic_slice_in_dim(value_new, first_group, shard_groups, 1),
            lengths,
        )
        attended = lax.all_to_all(attended.reshape(local_rows, heads_shard, head_dim), "model", 1, 0, tiled=True)
        partial = jnp.dot(attended.reshape(batch_all, heads_local * head_dim), w_out, preferred_element_type=jnp.float32)
        mixed_sum = lax.psum(partial, ("heads", "model"))
        out_tokens = (tokens.astype(jnp.float32) + mixed_sum).astype(jnp.bfloat16)
        return (out_tokens, key_new, value_new)

    cache_spec = P(("replica", "model"), None, None, None)
    new_spec = P(("replica", "model"), None, None)
    return jax.shard_map(
        local_step,
        mesh=mesh,
        in_specs=(P("replica", None), P(None, ("heads", "model")), P(None, None), P(None, None), P(("heads", "model"), None), cache_spec, cache_spec, P(("replica", "model"))),
        out_specs=(P("replica", None), new_spec, new_spec),
        check_vma=False,
    )
```

profile of v0, /device:TPU:0, one launch (start us, length us, event | category | flops | bytes accessed | tf_op | source)
XLA Modules:
  0.0 301.9 jit_solution(6013468517201024276)
XLA Ops:
  7.2 0.0 copy-start.1
  7.2 21.4 %convolution_convert_fusion = bf16[128,1536]{1,0:T(8,128)(2,1)S(1)} fusion(bf16[128,18432]{1,0:T(8,128)(2,1)} %param.8, bf16[18432,1536]{1,0:T(8,128)(2,1)} %param.9), kind=kOutput, calls=%fused_computation.14 | convolution fusion | flops 7247953920 | bytes 61734912 | tf_op jit(solution)/shard_map/dot_general | solution.py:37
  28.5 0.0 slice-start
  28.6 0.2 copy.23
  28.8 1.2 copy.24
  30.0 4.6 %all-to-all-start = ((bf16[128,6,256]{2,1,0:T(8,128)(2,1)}), bf16[128,6,256]{2,1,0:T(8,128)(2,1)S(1)}, u32[]{:S(2)}, u32[]{:S(2)}) async-start(bf16[128,6,256]{2,1,0:T(8,128)(2,1)} %copy.24), calls=%async_computation | async-start | bytes 1048576 | tf_op jit(solution)/shard_map/all_to_all | solution.py:38
  34.6 0.0 all-reduce.2.cloned.1.call-start
  34.6 0.0 copy-done.1
  34.6 0.1 iota_compare_fusion
  34.7 0.0 slice-start.1
  34.8 0.0 slice-start.2
  34.8 5.9 %convolution_convert_fusion.2 = bf16[32,256]{1,0:T(8,128)(2,1)S(1)} fusion(bf16[18432,256]{1,0:T(8,128)(2,1)} %param.10, bf16[128,18432]{1,0:T(8,128)(2,1)} %param.8, s32[]{:T(128)S(6)} %select_n.16), kind=kOutput, calls=%fused_computation.19 | convolution fusion | flops 301998080 | bytes 10633220 | tf_op jit(solution)/shard_map/dot_general | solution.py:40
  40.7 0.0 slice-done
  40.7 0.0 slice-done.1
  40.7 0.6 slice-done.2
  41.3 0.0 copy-start
  41.3 3.6 %fusion.38 = (f32[32,256]{1,0:T(8,128)S(1)}, bf16[32,256]{1,0:T(8,128)(2,1)}) fusion(bf16[18432,256]{1,0:T(8,128)(2,1)S(1)} %bitcast.37, bf16[128,18432]{1,0:T(8,128)(2,1)} %param.8, s32[]{:T(128)S(6)} %select_n.16), kind=kOutput, calls=%fused_computation.35 | convolution fusion | flops 302006272 | bytes 10665988 | tf_op jit(solution)/shard_map/dot_general | solution.py:42
  44.9 0.0 all-to-all-done
  44.9 0.1 copy.26
  45.0 0.3 fusion.29
  45.3 45.2 %fusion.4 = (f32[32,24]{1,0:T(8,128)S(1)}, f32[32,24,4096]{2,1,0:T(8,128)}) fusion(pred[32,4096]{1,0:T(8,128)(4,1)S(1)} %iota_compare_fusion, bf16[32,1,4096,256]{3,2,1,0:T(8,128)(2,1)} %param.13, bf16[32,24,256]{2,0,1:T(8,128)(2,1)S(1)} %bitcast.41), kind=kOutput, calls=%fused_computation.6 | convolution fusion | flops 1620049152 | bytes 80219136 | tf_op jit(solution)/shard_map/bgrd,bgtd->bgrt/dot_general | solution.py:9
  90.5 0.0 copy-done
  90.5 7.9 %fusion.5 = f32[32,24]{1,0:T(8,128)S(1)} fusion(f32[32,24,4096]{2,1,0:T(8,128)} %get-tuple-element.6, f32[32,24]{1,0:T(8,128)S(1)} %multiply_maximum_fusion, pred[32,4096]{1,0:T(8,128)(4,1)S(1)} %iota_compare_fusion), kind=kLoop, calls=%fused_computation.7 | loop fusion | flops 12582144 | bytes 12720128 | tf_op jit(solution)/shard_map/reduce_sum | solution.py:16
  98.5 26.8 %fusion.22 = bf16[32,24,256]{2,1,0:T(8,128)(2,1)S(1)} fusion(bf16[32,1,4096,256]{3,2,1,0:T(8,128)(2,1)} %param.14, f32[32,24,4096]{2,1,0:T(8,128)} %get-tuple-element.6, f32[32,24]{1,0:T(8,128)S(1)} %multiply_maximum_fusion, pred[32,4096]{1,0:T(8,128)(4,1)S(1)} %iota_compare_fusion, f32[32,24]{1,0:T(8,128)S(1)} %get-tuple-element.4, ...), kind=kOutput, calls=%fused_computation.17 | convolution fusion | flops 1623982080 | bytes 80258048 | tf_op jit(solution)/shard_map/bgrt,bgtd->bgrd/dot_general | solution.py:17
  125.3 0.1 copy.28
  125.4 10.7 %all_to_all.30 = bf16[32,24,256]{2,0,1:T(8,128)(2,1)S(1)} all-to-all(bf16[32,24,256]{2,0,1:T(8,128)(2,1)S(1)} %copy.28), channel_id=1, replica_groups=mesh['replica'=1,'heads'=2,'model'=4] {'model'}, dimensions={1} | all-to-all | bytes 786432 | tf_op jit(solution)/shard_map/all_to_all | solution.py:53
  136.1 0.2 copy.29
  136.4 0.1 copy.33
  136.5 23.7 %fusion.39 = f32[128,18432]{1,0:T(8,128)} fusion(bf16[128,1536]{1,0:T(8,128)(2,1)S(1)} %bitcast.42, bf16[1536,18432]{1,0:T(8,128)(2,1)} %param.12), kind=kOutput, calls=%fused_computation.36 | convolution fusion | flops 7247757312 | bytes 66453504 | tf_op jit(solution)/shard_map/dot_general | solution.py:54
  160.2 0.0 all-reduce.2.cloned.1.call-update
  160.2 126.7 %all-reduce.2.cloned.1.call-done = f32[128,18432]{1,0:T(8,128)} async-done(((f32[128,18432]{1,0:T(8,128)}), f32[128,18432]{1,0:T(8,128)}) %all-reduce.2.cloned.1.call-update) | async-done | bytes 9437200 | tf_op jit(solution)/shard_map/psum | solution.py:55
  286.9 8.1 %add_convert_fusion = bf16[128,18432]{1,0:T(8,128)(2,1)} fusion(f32[128,18432]{1,0:T(8,128)} %all-reduce.2.cloned.1.call-done, bf16[128,18432]{1,0:T(8,128)(2,1)} %param.8), kind=kLoop, calls=%fused_computation.9 | loop fusion | flops 7077888 | bytes 18874368 | tf_op jit(solution)/shard_map/convert_element_type | solution.py:56
  (3 shorter events, 0.0 us)
Async XLA Ops:
  7.2 27.4 %copy-start.1 = (s32[32]{0:T(128)S(1)}, s32[32]{0:T(128)}, u32[]{:S(2)}) copy-start(s32[32]{0:T(128)} %param.15) | copy-start | bytes 388
  28.5 12.1 %slice-start = ((s8[9437184]{0:T(1024)(128)(4,1)}), s8[1048576]{0:T(1024)(128)(4,1)S(1)}, s32[]{:S(2)}) async-start(s8[9437184]{0:T(1024)(128)(4,1)} %bitcast.36), calls=%async_computation.3 | async-start | bytes 2097152
  30.0 14.9 %all-to-all-start = ((bf16[128,6,256]{2,1,0:T(8,128)(2,1)}), bf16[128,6,256]{2,1,0:T(8,128)(2,1)S(1)}, u32[]{:S(2)}, u32[]{:S(2)}) async-start(bf16[128,6,256]{2,1,0:T(8,128)(2,1)} %copy.24), calls=%async_computation | async-start | bytes 1048576 | tf_op jit(solution)/shard_map/all_to_all | solution.py:38
  34.6 252.3 %all-reduce.2.cloned.1.call-start = ((), (), s32[]{:S(2)}) async-start(), calls=%async_computation.2 | async-start | bytes 18874368 | tf_op jit(solution)/shard_map/psum | solution.py:55
  34.7 5.9 %slice-start.1 = ((s8[9437184]{0:T(1024)(128)(4,1)}), s8[4194304]{0:T(1024)(128)(4,1)S(1)}, s32[]{:S(2)}) async-start(s8[9437184]{0:T(1024)(128)(4,1)} %bitcast.36), calls=%async_computation.4 | async-start | bytes 8388608
  34.8 6.5 %slice-start.2 = ((s8[9437184]{0:T(1024)(128)(4,1)}), s8[4194304]{0:T(1024)(128)(4,1)S(1)}, s32[]{:S(2)}) async-start(s8[9437184]{0:T(1024)(128)(4,1)} %bitcast.36), calls=%async_computation.5 | async-start | bytes 8388608
  41.3 49.3 %copy-start = (bf16[32,256]{1,0:T(8,128)(2,1)}, bf16[32,256]{1,0:T(8,128)(2,1)S(1)}, u32[]{:S(2)}) copy-start(bf16[32,256]{1,0:T(8,128)(2,1)S(1)} %convolution_convert_fusion.2) | copy-start | bytes 49156
Sparse Core Ops, SparseCore 0:
  160.3 126.5 all-reduce.1
where the time goes:
time: 302 us
  matrix products  127 us (42%)
  waiting for transfers between devices  127 us (42%)
  other arithmetic  16.2 us (5%)
  between operations  14.1 us (5%)
  blocking collectives  10.7 us (4%)
  starting transfers between devices  4.61 us (2%)
    psum x1, waiting for transfers between devices, local_step(): mixed_sum = lax.psum(partial, ('heads', 'model'))  127 us
    dot_general x1, matrix products, attend(): jnp.einsum('bgrd,bgtd->bgrt', queries, key_rows, preferred_element_type=j...  45.2 us
    dot_general x1, matrix products, attend(): jnp.einsum('bgrt,bgtd->bgrd', weights.astype(jnp.bfloat16), value_rows, p...  26.8 us
    dot_general x1, matrix products, local_step(): jnp.dot(attended.reshape(batch_all, heads_local * head_dim), w_out, prefe...  23.7 us
    dot_general x1, matrix products, local_step(): jnp.dot(tokens, w_query, preferred_element_type=jnp.float32)  21.4 us
    all_to_all x1, blocking collectives, local_step(): lax.all_to_all(attended.reshape(local_rows, heads_shard, head_dim), 'mode...  10.7 us
    convert_element_type x1, other arithmetic, local_step(): out_tokens = (tokens.astype(jnp.float32) + mixed_sum).astype(jnp.bfloat16)  8.13 us
    reduce_sum x1, other arithmetic, attend(): denom_sum = jnp.sum(weights, axis=-1) + weight_new  7.94 us
  transfers between devices with their start and end apart: 2, of which 1 were waited for; matrix products, arithmetic and copies ran while one was open for 3% of the time, Pallas kernels for 0%

commit v1 on v0

v1 whole, which is shorter than its diff:
```python
import functools

import jax
import jax.numpy as jnp
from jax import lax
from jax.experimental import pallas as pl
from jax.experimental.pallas import tpu as pltpu
from jax.sharding import PartitionSpec as P

MESH = pl.DeviceIdType.MESH
F32 = jnp.float32
BF16 = jnp.bfloat16
MIB = 1 << 20


def coordinates():
    y = lax.axis_index("heads")
    model = lax.axis_index("model")
    return y, model, model // 2, model % 2


def enter(others):
    y, model, _, _ = coordinates()
    me = y * 4 + model
    barrier = pltpu.get_barrier_semaphore()
    for offset in others:
        peer = (me + offset) % 8
        pl.semaphore_signal(barrier, inc=1, device_id={"heads": peer // 4, "model": peer % 4}, device_id_type=MESH)
    pl.semaphore_wait(barrier, len(others))


def query_kernel(groups, cols, depth, slots, kv_depth, kv_slots, x_ref, wq_ref, wk_ref, wv_ref, q_ref, kn_ref, vn_ref, wbuf, kvbuf, acc, kvacc, qs, kvs, kv_all,
                 w_sem, kv_sem, q_send, q_recv, kv_send, kv_recv, self_sem):
    y, model, _, _ = coordinates()
    me = y * 4 + model
    width = x_ref.shape[1]
    steps = width // depth
    kv_steps = width // kv_depth
    total = groups * steps

    def w_copy(i):
        g, k = i // steps, i % steps
        return pltpu.make_async_copy(wq_ref.at[pl.ds(k * depth, depth), pl.ds(g * cols, cols)], wbuf.at[i % slots], w_sem.at[i % slots])

    def kv_copy(ref, col, k):
        return pltpu.make_async_copy(ref.at[pl.ds(k * kv_depth, kv_depth), pl.ds(col * 128, 128)], kvbuf.at[k % kv_slots], kv_sem.at[k % kv_slots])

    def kv_start(k):
        @pl.when(model < 2)
        def _():
            kv_copy(wk_ref, model % 2, k).start()

        @pl.when(model >= 2)
        def _():
            kv_copy(wv_ref, model % 2, k).start()

    for k in range(kv_slots):
        kv_start(k)
    for i in range(slots):
        w_copy(i).start()

    enter(range(1, 8))

    kvacc[...] = jnp.zeros_like(kvacc)

    @pl.loop(0, kv_steps)
    def _(k):
        kv_copy(wk_ref, 0, k).wait()
        kvacc[...] += jnp.dot(x_ref[:, pl.ds(pl.multiple_of(k * kv_depth, 128), kv_depth)], kvbuf[k % kv_slots], preferred_element_type=F32)

        @pl.when(k + kv_slots < kv_steps)
        def _():
            kv_start(k + kv_slots)

    kvs[...] = kvacc[...].astype(BF16)

    def kv_send_copy(offset):
        peer = (model + offset) % 4
        return pltpu.make_async_remote_copy(
            src_ref=kvs.at[pl.ds(peer * 32, 32)], dst_ref=kv_all.at[model], send_sem=kv_send.at[offset], recv_sem=kv_recv.at[model],
            device_id={"heads": y, "model": peer}, device_id_type=MESH)

    for offset in range(1, 4):
        kv_send_copy(offset).start()
    kv_self = pltpu.make_async_copy(kvs.at[pl.ds(model * 32, 32)], kv_all.at[model], self_sem.at[0])
    kv_self.start()

    per_group = cols // 256

    def q_copy(g, h, offset):
        head = g * per_group + h
        peer = (me + offset) % 8
        rows = (peer % 4) * 2 + peer // 4
        return pltpu.make_async_remote_copy(
            src_ref=qs.at[head, pl.ds(rows * 16, 16)], dst_ref=q_ref.at[me * 6 + head],
            send_sem=q_send.at[head * 8 + offset], recv_sem=q_recv.at[me * 6 + head],
            device_id={"heads": peer // 4, "model": peer % 4}, device_id_type=MESH)

    def q_self(head):
        return pltpu.make_async_copy(qs.at[head, pl.ds((model * 2 + y) * 16, 16)], q_ref.at[me * 6 + head], self_sem.at[1 + head])

    @pl.loop(0, total)
    def _(i):
        g, k = i // steps, i % steps
        w_copy(i).wait()
        part = jnp.dot(x_ref[:, pl.ds(pl.multiple_of(k * depth, 128), depth)], wbuf[i % slots], preferred_element_type=F32)

        @pl.when(k == 0)
        def _():
            acc[...] = part

        @pl.when(k > 0)
        def _():
            acc[...] += part

        @pl.when(i + slots < total)
        def _():
            w_copy(i + slots).start()

        @pl.when(k == steps - 1)
        def _():
            for h in range(per_group):
                qs[g * per_group + h] = acc[:, h * 256:(h + 1) * 256].astype(BF16)
            for h in range(per_group):
                for offset in range(1, 8):
                    q_copy(g, h, offset).start()
                q_self(g * per_group + h).start()

    kv_self.wait()
    for offset in range(1, 4):
        kv_send_copy(offset).wait_send()
        src = (model + offset) % 4
        pltpu.make_async_copy(kv_all.at[src], kv_all.at[src], kv_recv.at[src]).wait()
    kn_ref[:, :128] = kv_all[0]
    kn_ref[:, 128:] = kv_all[1]
    vn_ref[:, :128] = kv_all[2]
    vn_ref[:, 128:] = kv_all[3]

    @pl.loop(0, 6)
    def _(head):
        q_self(head).wait()
        for offset in range(1, 8):
            q_copy(0, head, offset).wait_send()
            src = (me + offset) % 8
            pltpu.make_async_copy(q_ref.at[src * 6 + head], q_ref.at[src * 6 + head], q_recv.at[src * 6 + head]).wait()


def project_queries(tokens, w_query, w_key, w_value):
    rows, width = tokens.shape
    groups, cols, depth, slots = 3, 512, 2304, 6
    kv_depth, kv_slots = 4608, 2
    vmem = pl.BlockSpec(memory_space=pltpu.VMEM)
    hbm = pl.BlockSpec(memory_space=pl.ANY)
    return pl.pallas_call(
        functools.partial(query_kernel, groups, cols, depth, slots, kv_depth, kv_slots),
        out_shape=(jax.ShapeDtypeStruct((48, 16, 256), BF16), jax.ShapeDtypeStruct((32, 256), BF16), jax.ShapeDtypeStruct((32, 256), BF16)),
        in_specs=[vmem, hbm, hbm, hbm],
        out_specs=(vmem, vmem, vmem),
        scratch_shapes=[
            pltpu.VMEM((slots, depth, cols), BF16),
            pltpu.VMEM((kv_slots, kv_depth, 128), BF16),
            pltpu.VMEM((rows, cols), F32),
            pltpu.VMEM((rows, 128), F32),
            pltpu.VMEM((6, rows, 256), BF16),
            pltpu.VMEM((rows, 128), BF16),
            pltpu.VMEM((4, 32, 128), BF16),
            pltpu.SemaphoreType.DMA((slots,)),
            pltpu.SemaphoreType.DMA((kv_slots,)),
            pltpu.SemaphoreType.DMA((48,)),
            pltpu.SemaphoreType.DMA((48,)),
            pltpu.SemaphoreType.DMA((4,)),
            pltpu.SemaphoreType.DMA((4,)),
            pltpu.SemaphoreType.DMA((7,)),
        ],
        compiler_params=pltpu.CompilerParams(collective_id=0, has_side_effects=True, vmem_limit_bytes=48 * MIB),
        cost_estimate=pl.CostEstimate(flops=2 * rows * width * 1664, bytes_accessed=width * 1664 * 2, transcendentals=0),
        name="query",
    )(tokens, w_query, w_key, w_value)


ITEM = 1024


def attend_kernel(slots, len_ref, q_ref, kn_ref, vn_ref, key_ref, value_ref, o_ref, kbuf, vbuf, qf, of, knf, vnf, sbuf, acc, m_ref, l_ref, items, k_sem, v_sem):
    y = lax.axis_index("heads")
    first_seq = y * 16
    scale = 256 ** -0.5

    def list_seq(s, count):
        length = len_ref[first_seq + s]
        chunks = (length + ITEM - 1) // ITEM
        for c in range(4):
            @pl.when(c < chunks)
            def _():
                items[count + c] = s * 4 + c
        return count + chunks

    total = lax.fori_loop(0, 16, list_seq, jnp.int32(0))

    def where_is(i):
        entry = items[i]
        s, c = entry // 4, entry % 4
        left = jnp.minimum(len_ref[first_seq + s] - c * ITEM, ITEM)
        return s, c, pl.multiple_of((left + 15) // 16 * 16, 16)

    def copy(i, ref, buf, sem):
        s, c, size = where_is(i)
        slot = i % slots
        return pltpu.make_async_copy(ref.at[first_seq + s, 0, pl.ds(pl.multiple_of(c * ITEM, ITEM), size)], buf.at[slot, pl.ds(0, size)], sem.at[slot])

    def k_copy(i):
        return copy(i, key_ref, kbuf, k_sem)

    def v_copy(i):
        return copy(i, value_ref, vbuf, v_sem)

    for i in range(slots - 1):
        @pl.when(i < total)
        def _():
            k_copy(i).start()
    for i in range(slots):
        vbuf[i] = jnp.zeros((ITEM, 256), BF16)
        if i < slots - 1:
            @pl.when(i < total)
            def _():
                v_copy(i).start()

    for part in range(2):
        qf[part] = q_ref[:, :, part * 128:(part + 1) * 128].reshape(768, 128).astype(F32)
    knf[...] = kn_ref[...].astype(F32)
    vnf[...] = vn_ref[...].astype(F32)
    m_ref[...] = jnp.zeros_like(m_ref)
    l_ref[...] = jnp.ones_like(l_ref)
    acc[...] = jnp.zeros_like(acc)

    def query(s):
        return jnp.concatenate([qf[part, pl.ds(s, 48, stride=16), :] for part in range(2)], axis=1)

    def scores(i):
        s, _, _ = where_is(i)
        q = query(s).astype(BF16)
        sbuf[i % 2] = lax.dot_general(q, kbuf[i % slots], (((1,), (1,)), ((), ())), preferred_element_type=F32)

    k_copy(0).wait()
    scores(0)

    @pl.loop(0, total)
    def _(i):
        @pl.when(i + slots - 1 < total)
        def _():
            k_copy(i + slots - 1).start()
            v_copy(i + slots - 1).start()

        after = jnp.minimum(i + 1, total - 1)

        @pl.when(i + 1 < total)
        def _():
            k_copy(i + 1).wait()
        v_copy(i).wait()

        s_after, _, _ = where_is(after)
        q_after = query(s_after).astype(BF16)
        s_next = lax.dot_general(q_after, kbuf[after % slots], (((1,), (1,)), ((), ())), preferred_element_type=F32)

        s, c, _ = where_is(i)
        left = len_ref[first_seq + s] - c * ITEM
        fresh = c == 0
        q_now = query(s)
        kn = knf[pl.ds(first_seq + s, 1), :]
        vn = vnf[pl.ds(first_seq + s, 1), :]
        score_new = jnp.sum(q_now * kn, axis=1, keepdims=True) * scale
        m_old = jnp.where(fresh, score_new, m_ref[:, :1])
        l_old = jnp.where(fresh, 1.0, l_ref[:, :1])
        acc_old = jnp.where(fresh, jnp.broadcast_to(vn, acc.shape), acc[...])
        x = sbuf[i % 2] * scale
        x = jnp.where(lax.broadcasted_iota(jnp.int32, x.shape, 1) < left, x, -jnp.inf)
        m_now = jnp.maximum(m_old, jnp.max(x, axis=1, keepdims=True))
        alpha = jnp.exp(m_old - m_now)
        p = jnp.exp(x - m_now)
        l_now = l_old * alpha + jnp.sum(p, axis=1, keepdims=True)
        acc_now = acc_old * alpha + jnp.dot(p.astype(BF16), vbuf[i % slots], preferred_element_type=F32)
        m_ref[...] = jnp.broadcast_to(m_now, m_ref.shape)
        l_ref[...] = jnp.broadcast_to(l_now, l_ref.shape)
        acc[...] = acc_now
        result = acc_now / l_now
        for part in range(2):
            of[part, pl.ds(pl.multiple_of(s * 48, 8), 48), :] = result[:, part * 128:(part + 1) * 128]
        sbuf[(i + 1) % 2] = s_next

    for h in range(48):
        for part in range(2):
            start = (h % 6) * 256 + part * 128
            o_ref[h // 6, :, start:start + 128] = of[part, pl.ds(h, 16, stride=48), :].astype(BF16)


def attend(lengths, queries, key_new, value_new, key_cache, value_cache):
    slots = 10
    vmem = pl.BlockSpec(memory_space=pltpu.VMEM)
    hbm = pl.BlockSpec(memory_space=pl.ANY)
    return pl.pallas_call(
        functools.partial(attend_kernel, slots),
        out_shape=jax.ShapeDtypeStruct((8, 16, 1536), BF16),
        in_specs=[pl.BlockSpec(memory_space=pltpu.SMEM), vmem, vmem, vmem, hbm, hbm],
        out_specs=vmem,
        scratch_shapes=[
            pltpu.VMEM((slots, ITEM, 256), BF16),
            pltpu.VMEM((slots, ITEM, 256), BF16),
            pltpu.VMEM((2, 768, 128), F32),
            pltpu.VMEM((2, 768, 128), F32),
            pltpu.VMEM((32, 256), F32),
            pltpu.VMEM((32, 256), F32),
            pltpu.VMEM((2, 48, ITEM), F32),
            pltpu.VMEM((48, 256), F32),
            pltpu.VMEM((48, 128), F32),
            pltpu.VMEM((48, 128), F32),
            pltpu.SMEM((64,), jnp.int32),
            pltpu.SemaphoreType.DMA((slots,)),
            pltpu.SemaphoreType.DMA((slots,)),
        ],
        compiler_params=pltpu.CompilerParams(vmem_limit_bytes=40 * MIB),
        cost_estimate=pl.CostEstimate(flops=4 * 16 * 48 * 2048 * 256, bytes_accessed=16 * 2048 * 1024, transcendentals=16 * 48 * 2048),
        name="attend",
    )(lengths, queries, key_new, value_new, key_cache, value_cache)


LAGS = (1, 4, 7, 10, 13)


def mix_kernel(chunk, slots, o_ref, w_ref, x_ref, out_ref, o_all, wbuf, xrows, part, r0, r1, r2,
               w_sem, x_sem, o_send, o_recv, s0s, s0r, s1s, s1r, s2s, s2r, g1s, g1r, g2s, g2r, g3s, g3r):
    y, model, x, core = coordinates()
    me = y * 4 + model
    width = w_ref.shape[1]
    chunks = width // chunk
    first, second = x * (1 - core) + y * core, y * (1 - core) + x * core
    own = core * 4 + first * 2 + second
    flip_x = {"heads": y, "model": (1 - x) * 2 + core}
    partner = {"heads": y, "model": x * 2 + 1 - core}
    along_first = {"heads": y * (1 - core) + (1 - y) * core, "model": ((1 - x) * (1 - core) + x * core) * 2 + core}
    along_second = {"heads": (1 - y) * (1 - core) + y * core, "model": (x * (1 - core) + (1 - x) * core) * 2 + core}

    def w_copy(t):
        return pltpu.make_async_copy(w_ref.at[:, pl.ds(pl.multiple_of(t * chunk, chunk), chunk)], wbuf.at[t % slots], w_sem.at[t % slots])

    for t in range(slots):
        w_copy(t).start()
    x_copy = pltpu.make_async_copy(x_ref.at[pl.ds(own * 16, 16)], xrows, x_sem)
    x_copy.start()

    enter(range(1, 8))

    mine = model * 2 + y

    def o_copy(offset):
        peer = (me + offset) % 8
        return pltpu.make_async_remote_copy(
            src_ref=o_ref.at[peer], dst_ref=o_all.at[pl.ds(mine * 16, 16)], send_sem=o_send.at[offset], recv_sem=o_recv.at[me],
            device_id={"heads": peer // 4, "model": peer % 4}, device_id_type=MESH)

    for offset in range(1, 8):
        o_copy(offset).start()
    o_self = pltpu.make_async_copy(o_ref.at[me], o_all.at[pl.ds(mine * 16, 16)], o_send.at[0])
    o_self.start()
    o_self.wait()
    for offset in range(1, 8):
        src = (me + offset) % 8
        block = o_all.at[pl.ds(((src % 4) * 2 + src // 4) * 16, 16)]
        pltpu.make_async_copy(block, block, o_recv.at[src]).wait()
    x_copy.wait()

    def remote(src, dst, send, recv, device):
        return pltpu.make_async_remote_copy(src_ref=src, dst_ref=dst, send_sem=send, recv_sem=recv, device_id=device, device_id_type=MESH)

    half, quarter = core * 64, core * 64 + first * 32
    eighth = quarter + second * 16
    cols = lambda j: pl.ds(pl.multiple_of(j * chunk, chunk), chunk)

    def s0(j):
        return remote(part.at[j, pl.ds((1 - core) * 64, 64)], r0.at[j], s0s.at[j], s0r.at[j], partner)

    def s1(j):
        return remote(part.at[j, pl.ds(half + (1 - first) * 32, 32)], r1.at[j], s1s.at[j], s1r.at[j], along_first)

    def s2(j):
        return remote(part.at[j, pl.ds(quarter + (1 - second) * 16, 16)], r2.at[j], s2s.at[j], s2r.at[j], along_second)

    def g1(j):
        piece = out_ref.at[pl.ds(eighth, 16), cols(j)]
        return remote(piece, piece, g1s.at[j], g1r.at[j], along_second)

    def g2(j):
        piece = out_ref.at[pl.ds(quarter, 32), cols(j)]
        return remote(piece, piece, g2s.at[j], g2r.at[j], along_first)

    def g3(j):
        piece = out_ref.at[pl.ds(half, 64), cols(j)]
        return remote(piece, piece, g3s.at[j], g3r.at[j], partner)

    def arrived(ref, sem):
        pltpu.make_async_copy(ref, ref, sem).wait()

    def at(t, lag, body):
        j = t - lag

        @pl.when(jnp.logical_and(j >= 0, j < chunks))
        def _():
            body(j)

    def stage5(j):
        arrived(out_ref.at[pl.ds(core * 64 + (1 - first) * 32, 32), cols(j)], g2r.at[j])
        g3(j).start()

    def stage4(j):
        arrived(out_ref.at[pl.ds(quarter + (1 - second) * 16, 16), cols(j)], g1r.at[j])
        g2(j).start()

    def stage3(j):
        arrived(r2.at[j], s2r.at[j])
        total = part[j, pl.ds(pl.multiple_of(eighth, 16), 16)] + r2[j]
        out_ref[pl.ds(pl.multiple_of(eighth, 16), 16), cols(j)] = (xrows[:, cols(j)].astype(F32) + total).astype(BF16)
        g1(j).start()

    def stage2(j):
        arrived(r1.at[j], s1r.at[j])
        part[j, pl.ds(pl.multiple_of(quarter, 16), 32)] += r1[j]
        s2(j).start()

    def stage1(j):
        arrived(r0.at[j], s0r.at[j])
        part[j, pl.ds(pl.multiple_of(half, 16), 64)] += r0[j]
        s1(j).start()

    def stage0(j):
        w_copy(j).wait()
        part[j] = jnp.dot(o_all[...], wbuf[j % slots], preferred_element_type=F32)

        @pl.when(j + slots < chunks)
        def _():
            w_copy(j + slots).start()
        s0(j).start()

    @pl.loop(0, chunks + LAGS[-1])
    def _(t):
        at(t, 0, stage0)
        at(t, LAGS[0], stage1)
        at(t, LAGS[1], stage2)
        at(t, LAGS[2], stage3)
        at(t, LAGS[3], stage4)
        at(t, LAGS[4], stage5)

    for offset in range(1, 8):
        o_copy(offset).wait_send()

    @pl.loop(0, chunks)
    def _(j):
        arrived(out_ref.at[pl.ds((1 - core) * 64, 64), cols(j)], g3r.at[j])
        for copy in (s0, s1, s2, g1, g2, g3):
            copy(j).wait_send()


def mix(attended, w_out, tokens):
    depth, width = w_out.shape
    chunk, slots = 512, 8
    chunks = width // chunk
    vmem = pl.BlockSpec(memory_space=pltpu.VMEM)
    hbm = pl.BlockSpec(memory_space=pl.ANY)
    sems = pltpu.SemaphoreType.DMA((chunks,))
    return pl.pallas_call(
        functools.partial(mix_kernel, chunk, slots),
        out_shape=jax.ShapeDtypeStruct((128, width), BF16),
        in_specs=[vmem, hbm, hbm],
        out_specs=vmem,
        scratch_shapes=[
            pltpu.VMEM((128, depth), BF16),
            pltpu.VMEM((slots, depth, chunk), BF16),
            pltpu.VMEM((16, width), BF16),
            pltpu.VMEM((chunks, 128, chunk), F32),
            pltpu.VMEM((chunks, 64, chunk), F32),
            pltpu.VMEM((chunks, 32, chunk), F32),
            pltpu.VMEM((chunks, 16, chunk), F32),
            pltpu.SemaphoreType.DMA((slots,)),
            pltpu.SemaphoreType.DMA,
            pltpu.SemaphoreType.DMA((8,)),
            pltpu.SemaphoreType.DMA((8,)),
        ] + [sems] * 12,
        compiler_params=pltpu.CompilerParams(collective_id=1, has_side_effects=True, vmem_limit_bytes=56 * MIB),
        cost_estimate=pl.CostEstimate(flops=2 * 128 * depth * width, bytes_accessed=depth * width * 2, transcendentals=0),
        name="mix",
    )(attended, w_out, tokens)


def solution(mesh):
    def local_step(tokens, w_query, w_key, w_value, w_out, key_cache, value_cache, lengths):
        queries, key_new, value_new = project_queries(tokens, w_query, w_key, w_value)
        attended = attend(lengths, queries, key_new, value_new, key_cache, value_cache)
        out_tokens = mix(attended, w_out, tokens)
        return (out_tokens, key_new.reshape(32, 1, 256), value_new.reshape(32, 1, 256))

    cache_spec = P(("replica", "model"), None, None, None)
    new_spec = P(("replica", "model"), None, None)
    return jax.shard_map(
        local_step,
        mesh=mesh,
        in_specs=(P("replica", None), P(None, ("heads", "model")), P(None, None), P(None, None), P(("heads", "model"), None), cache_spec, cache_spec, P(("replica", "model"))),
        out_specs=(P("replica", None), new_spec, new_spec),
        check_vma=False,
    )
```

time: 302 us -> 149 us (0.49)
  Pallas kernels: 0 us -> 138 us
  matrix products: 127 us -> 0 us
  waiting for transfers between devices: 127 us -> 0 us
  other arithmetic: 16.2 us -> 0 us
  between operations: 14.1 us -> 0.68 us
  blocking collectives: 10.7 us -> 0 us
  local copies, waits for them, and re-layouts: 2.47 us -> 9.23 us
  starting transfers between devices: 4.61 us -> 0 us
    pallas_call x0 -> x3, Pallas kernels: none -> 138 us  [the longest x1 85.5 us: mix(): pl.pallas_call(functools.partial(mix_kernel, chunk, slots), out_shape=jax...]
    dot_general x7 -> x0, matrix products: 127 us -> none  [the longest x1 45.2 us: attend(): jnp.einsum('bgrd,bgtd->bgrt', queries, key_rows, preferred_element_type=j...]
    psum x1 -> x0, waiting for transfers between devices: 127 us -> none  [local_step(): mixed_sum = lax.psum(partial, ('heads', 'model'))]
    all_to_all x1 -> x0, blocking collectives: 10.7 us -> none  [local_step(): lax.all_to_all(attended.reshape(local_rows, heads_shard, head_dim), 'mode...]
    unnamed x11 -> x9, local copies, waits for them, and re-layouts: 0.67 us -> 9.23 us
    convert_element_type x2 -> x0, other arithmetic: 8.15 us -> none  [the longest x1 8.13 us: local_step(): out_tokens = (tokens.astype(jnp.float32) + mixed_sum).astype(jnp.bfloat16)]
    reduce_sum x1 -> x0, other arithmetic: 7.94 us -> none  [attend(): denom_sum = jnp.sum(weights, axis=-1) + weight_new]
    all_to_all x1 -> x0, starting transfers between devices: 4.61 us -> none  [local_step(): lax.all_to_all(queries.reshape(batch_all, heads_local, head_dim), 'model'...]
  transfers between devices with their start and end apart: 2 -> 0, of which waited for: 1 -> 0; matrix products, arithmetic and copies ran while one was open for 3% -> 0% of each run, Pallas kernels for 0% -> 0%
where the time goes in v1:
time: 149 us; the launch traced here: 148 us
  Pallas kernels  138 us (93%)
  local copies, waits for them, and re-layouts  9.23 us (6%)
    pallas_call x1, Pallas kernels, mix(): pl.pallas_call(functools.partial(mix_kernel, chunk, slots), out_shape=jax...  85.5 us
    pallas_call x1, Pallas kernels, project_queries(): pl.pallas_call(functools.partial(query_kernel, groups, cols, depth, slots...  29.5 us
    pallas_call x1, Pallas kernels, attend(): pl.pallas_call(functools.partial(attend_kernel, slots), out_shape=jax.Sha...  23.2 us
    unnamed x9, local copies, waits for them, and re-layouts  9.23 us

profile of v1, /device:TPU:0, one launch (start us, length us, event | category | flops | bytes accessed | tf_op | source)
XLA Modules:
  0.0 148.1 jit_solution(2044074263265206615)
XLA Ops:
  0.6 0.0 copy-start
  0.6 2.3 %copy-done = bf16[128,18432]{1,0:T(8,128)(2,1)S(1)} copy-done((bf16[128,18432]{1,0:T(8,128)(2,1)S(1)}, bf16[128,18432]{1,0:T(8,128)(2,1)}, u32[]{:S(2)}) %copy-start) | copy-done | bytes 4718616
  3.0 0.0 copy-start.2
  3.0 29.5 %query.1 = (bf16[48,16,256]{2,1,0:T(8,128)(2,1)S(1)}, bf16[32,256]{1,0:T(8,128)(2,1)S(1)}, bf16[32,256]{1,0:T(8,128)(2,1)S(1)}) custom-call(bf16[128,18432]{1,0:T(8,128)(2,1)S(1)} %copy-done, bf16[18432,1536]{1,0:T(8,128)(2,1)} %wq_ref.1, bf16[18432,256]{1,0:T(8,128)(2,1)} %wk_ref.1, bf16[18432,256]{1,0:T(8,128)(2,1)} %wv_ref.1), custom_call_target="tpu_custom_call" | custom-call | flops 7851737088 | bytes 61341696 | tf_op jit(solution)/shard_map/query/pallas_call | solution.py:154
  32.5 0.0 copy-done.2
  32.5 23.2 %attend.1.o_ref = bf16[8,16,1536]{2,1,0:T(8,128)(2,1)S(1)} custom-call(s32[32]{0:T(128)S(1)} %copy-done.2, bf16[48,16,256]{2,1,0:T(8,128)(2,1)S(1)} %get-tuple-element.6.q_ref, bf16[32,256]{1,0:T(8,128)(2,1)S(1)} %get-tuple-element.7.kn_ref, bf16[32,256]{1,0:T(8,128)(2,1)S(1)} %get-tuple-element.8.vn_ref, bf16[32,1,4096,256]{3,2,1,0:T(8,128)(2,1)} %key_ref.1, ...), custom_call_target="tpu_custom_call" | custom-call | flops 1610612736 | bytes 33554432 | tf_op jit(solution)/shard_map/attend/pallas_call | solution.py:300
  55.7 0.0 copy-start.1
  55.7 0.7 copy-done.1
  56.4 85.5 %mix.1 = bf16[128,18432]{1,0:T(8,128)(2,1)} custom-call(bf16[8,16,1536]{2,1,0:T(8,128)(2,1)} %copy-done.1, bf16[1536,18432]{1,0:T(8,128)(2,1)} %w_ref.1, bf16[128,18432]{1,0:T(8,128)(2,1)} %x_ref.3), custom_call_target="tpu_custom_call" | custom-call | flops 7247757312 | bytes 56623104 | tf_op jit(solution)/shard_map/mix/pallas_call | solution.py:468
  141.9 4.9 %copy.14 = bf16[128,18432]{1,0:T(8,128)(2,1)} copy(bf16[128,18432]{1,0:T(8,128)(2,1)} %mix.1) | data formatting | bytes 9437184
  146.9 0.6 copy.15
  147.5 0.6 copy.16
Async XLA Ops:
  0.6 2.3 %copy-start = (bf16[128,18432]{1,0:T(8,128)(2,1)S(1)}, bf16[128,18432]{1,0:T(8,128)(2,1)}, u32[]{:S(2)}) copy-start(bf16[128,18432]{1,0:T(8,128)(2,1)} %x_ref.3) | copy-start | bytes 14155780
  3.0 29.5 %copy-start.2 = (s32[32]{0:T(128)S(1)}, s32[32]{0:T(128)}, u32[]{:S(2)}) copy-start(s32[32]{0:T(128)} %len_ref.1) | copy-start | bytes 388
  55.7 0.7 copy-start.1

commit v2 on v1

--- a/solution.py
+++ b/solution.py
@@ -29,8 +29,8 @@
     pl.semaphore_wait(barrier, len(others))
 
 
-def query_kernel(groups, cols, depth, slots, kv_depth, kv_slots, x_ref, wq_ref, wk_ref, wv_ref, q_ref, kn_ref, vn_ref, wbuf, kvbuf, acc, kvacc, qs, kvs, kv_all,
-                 w_sem, kv_sem, q_send, q_recv, kv_send, kv_recv, self_sem):
+def query_kernel(groups, cols, depth, slots, kv_depth, x_ref, wq_ref, wk_ref, wv_ref, q_ref, kn_ref, vn_ref, xbuf, wbuf, kvbuf, acc, kvacc, qs, kvs, kv_all,
+                 x_sem, w_sem, kv_sem, q_send, q_recv, kv_send, kv_recv, self_sem):
     y, model, _, _ = coordinates()
     me = y * 4 + model
     width = x_ref.shape[1]
@@ -42,48 +42,20 @@
         g, k = i // steps, i % steps
         return pltpu.make_async_copy(wq_ref.at[pl.ds(k * depth, depth), pl.ds(g * cols, cols)], wbuf.at[i % slots], w_sem.at[i % slots])
 
+    def x_copy(k):
+        part = pl.ds(pl.multiple_of(k * depth, 128), depth)
+        return pltpu.make_async_copy(x_ref.at[:, part], xbuf.at[:, part], x_sem.at[k])
+
     def kv_copy(ref, col, k):
-        return pltpu.make_async_copy(ref.at[pl.ds(k * kv_depth, kv_depth), pl.ds(col * 128, 128)], kvbuf.at[k % kv_slots], kv_sem.at[k % kv_slots])
-
-    def kv_start(k):
-        @pl.when(model < 2)
-        def _():
-            kv_copy(wk_ref, model % 2, k).start()
-
-        @pl.when(model >= 2)
-        def _():
-            kv_copy(wv_ref, model % 2, k).start()
-
-    for k in range(kv_slots):
-        kv_start(k)
-    for i in range(slots):
-        w_copy(i).start()
+        return pltpu.make_async_copy(ref.at[pl.ds(k * kv_depth, kv_depth), pl.ds(col * 128, 128)], kvbuf.at[k], kv_sem.at[k])
+
+    for i in range(max(steps, slots)):
+        if i < steps:
+            x_copy(i).start()
+        if i < slots:
+            w_copy(i).start()
 
     enter(range(1, 8))
-
-    kvacc[...] = jnp.zeros_like(kvacc)
-
-    @pl.loop(0, kv_steps)
-    def _(k):
-        kv_copy(wk_ref, 0, k).wait()
-        kvacc[...] += jnp.dot(x_ref[:, pl.ds(pl.multiple_of(k * kv_depth, 128), kv_depth)], kvbuf[k % kv_slots], preferred_element_type=F32)
-
-        @pl.when(k + kv_slots < kv_steps)
-        def _():
-            kv_start(k + kv_slots)
-
-    kvs[...] = kvacc[...].astype(BF16)
-
-    def kv_send_copy(offset):
-        peer = (model + offset) % 4
-        return pltpu.make_async_remote_copy(
-            src_ref=kvs.at[pl.ds(peer * 32, 32)], dst_ref=kv_all.at[model], send_sem=kv_send.at[offset], recv_sem=kv_recv.at[model],
-            device_id={"heads": y, "model": peer}, device_id_type=MESH)
-
-    for offset in range(1, 4):
-        kv_send_copy(offset).start()
-    kv_self = pltpu.make_async_copy(kvs.at[pl.ds(model * 32, 32)], kv_all.at[model], self_sem.at[0])
-    kv_self.start()
 
     per_group = cols // 256
 
@@ -102,8 +74,13 @@
     @pl.loop(0, total)
     def _(i):
         g, k = i // steps, i % steps
+
+        @pl.when(i < steps)
+        def _():
+            x_copy(i).wait()
+
         w_copy(i).wait()
-        part = jnp.dot(x_ref[:, pl.ds(pl.multiple_of(k * depth, 128), depth)], wbuf[i % slots], preferred_element_type=F32)
+        part = jnp.dot(xbuf[:, pl.ds(pl.multiple_of(k * depth, 128), depth)], wbuf[i % slots], preferred_element_type=F32)
 
         @pl.when(k == 0)
         def _():
@@ -116,15 +93,54 @@
         @pl.when(i + slots < total)
         def _():
             w_copy(i + slots).start()
+
+        for n in range(kv_steps):
+            @pl.when(i == total - kv_steps + n - 1)
+            def _():
+                @pl.when(model < 2)
+                def _():
+                    kv_copy(wk_ref, model % 2, n).start()
+
+                @pl.when(model >= 2)
+                def _():
+                    kv_copy(wv_ref, model % 2, n).start()
 
         @pl.when(k == steps - 1)
         def _():
             for h in range(per_group):
                 qs[g * per_group + h] = acc[:, h * 256:(h + 1) * 256].astype(BF16)
             for h in range(per_group):
-                for offset in range(1, 8):
+                for offset in (7, 6, 5, 4, 3, 2, 1):
                     q_copy(g, h, offset).start()
                 q_self(g * per_group + h).start()
+
+    kvacc[...] = jnp.zeros_like(kvacc)
+
+    @pl.loop(0, kv_steps)
+    def _(k):
+        kv_copy(wk_ref, 0, k).wait()
+        kvacc[...] += jnp.dot(xbuf[:, pl.ds(pl.multiple_of(k * kv_depth, 128), kv_depth)], kvbuf[k], preferred_element_type=F32)
+
+    kvs[...] = kvacc[...].astype(BF16)
+
+    def kv_send_copy(offset):
+        peer = (model + offset) % 4
+        return pltpu.make_async_remote_copy(
+            src_ref=kvs.at[pl.ds(peer * 32, 32)], dst_ref=kv_all.at[model], send_sem=kv_send.at[offset], recv_sem=kv_recv.at[model],
+            device_id={"heads": y, "model": peer}, device_id_type=MESH)
+
+    for offset in (2, 3, 1):
+        kv_send_copy(offset).start()
+    kv_self = pltpu.make_async_copy(kvs.at[pl.ds(model * 32, 32)], kv_all.at[model], self_sem.at[0])
+    kv_self.start()
+
+    @pl.loop(0, 6)
+    def _(head):
+        q_self(head).wait()
+        for offset in range(1, 8):
+            q_copy(0, head, offset).wait_send()
+            src = (me + offset) % 8
+            pltpu.make_async_copy(q_ref.at[src * 6 + head], q_ref.at[src * 6 + head], q_recv.at[src * 6 + head]).wait()
 
     kv_self.wait()
     for offset in range(1, 4):
@@ -136,36 +152,30 @@
     vn_ref[:, :128] = kv_all[2]
     vn_ref[:, 128:] = kv_all[3]
 
-    @pl.loop(0, 6)
-    def _(head):
-        q_self(head).wait()
-        for offset in range(1, 8):
-            q_copy(0, head, offset).wait_send()
-            src = (me + offset) % 8
-            pltpu.make_async_copy(q_ref.at[src * 6 + head], q_ref.at[src * 6 + head], q_recv.at[src * 6 + head]).wait()
-
 
 def project_queries(tokens, w_query, w_key, w_value):
     rows, width = tokens.shape
-    groups, cols, depth, slots = 3, 512, 2304, 6
-    kv_depth, kv_slots = 4608, 2
+    groups, cols, depth, slots = 6, 256, 4608, 6
+    kv_depth = 4608
     vmem = pl.BlockSpec(memory_space=pltpu.VMEM)
-    hbm = pl.BlockSpec(memory_space=pl.ANY)
+    hbm = pl.BlockSpec(memory_space=pltpu.HBM)
     return pl.pallas_call(
-        functools.partial(query_kernel, groups, cols, depth, slots, kv_depth, kv_slots),
+        functools.partial(query_kernel, groups, cols, depth, slots, kv_depth),
         out_shape=(jax.ShapeDtypeStruct((48, 16, 256), BF16), jax.ShapeDtypeStruct((32, 256), BF16), jax.ShapeDtypeStruct((32, 256), BF16)),
-        in_specs=[vmem, hbm, hbm, hbm],
+        in_specs=[hbm, hbm, hbm, hbm],
         out_specs=(vmem, vmem, vmem),
         scratch_shapes=[
+            pltpu.VMEM((rows, width), BF16),
             pltpu.VMEM((slots, depth, cols), BF16),
-            pltpu.VMEM((kv_slots, kv_depth, 128), BF16),
+            pltpu.VMEM((width // kv_depth, kv_depth, 128), BF16),
             pltpu.VMEM((rows, cols), F32),
             pltpu.VMEM((rows, 128), F32),
             pltpu.VMEM((6, rows, 256), BF16),
             pltpu.VMEM((rows, 128), BF16),
             pltpu.VMEM((4, 32, 128), BF16),
+            pltpu.SemaphoreType.DMA((width // depth,)),
             pltpu.SemaphoreType.DMA((slots,)),
-            pltpu.SemaphoreType.DMA((kv_slots,)),
+            pltpu.SemaphoreType.DMA((width // kv_depth,)),
             pltpu.SemaphoreType.DMA((48,)),
             pltpu.SemaphoreType.DMA((48,)),
             pltpu.SemaphoreType.DMA((4,)),
@@ -175,16 +185,16 @@
         compiler_params=pltpu.CompilerParams(collective_id=0, has_side_effects=True, vmem_limit_bytes=48 * MIB),
         cost_estimate=pl.CostEstimate(flops=2 * rows * width * 1664, bytes_accessed=width * 1664 * 2, transcendentals=0),
         name="query",
-    )(tokens, w_query, w_key, w_value)
+    )(*(pltpu.with_memory_space_constraint(a, pltpu.HBM) for a in (tokens, w_query, w_key, w_value)))
 
 
 ITEM = 1024
 
 
-def attend_kernel(slots, len_ref, q_ref, kn_ref, vn_ref, key_ref, value_ref, o_ref, kbuf, vbuf, qf, of, knf, vnf, sbuf, acc, m_ref, l_ref, items, k_sem, v_sem):
+def attend_kernel(slots, len_ref, q_ref, kn_ref, vn_ref, key_ref, value_ref, o_ref, kn_out, vn_out, kbuf, vbuf, perm, back, qs, os, sn, vnf, sbuf, pbuf, acc, m_ref, l_ref, a_ref, r_ref, items, left, k_sem, v_sem):
     y = lax.axis_index("heads")
     first_seq = y * 16
-    scale = 256 ** -0.5
+    power = 256 ** -0.5 * 1.4426950408889634
 
     def list_seq(s, count):
         length = len_ref[first_seq + s]
@@ -193,20 +203,19 @@
             @pl.when(c < chunks)
             def _():
                 items[count + c] = s * 4 + c
+                left[count + c] = length - c * ITEM
         return count + chunks
 
     total = lax.fori_loop(0, 16, list_seq, jnp.int32(0))
-
-    def where_is(i):
+    items[total] = items[total - 1] // 4 * 4 + 3
+    left[total] = 0
+    pairs = (total + 1) // 2
+
+    def copy(i, ref, buf, sem):
         entry = items[i]
-        s, c = entry // 4, entry % 4
-        left = jnp.minimum(len_ref[first_seq + s] - c * ITEM, ITEM)
-        return s, c, pl.multiple_of((left + 15) // 16 * 16, 16)
-
-    def copy(i, ref, buf, sem):
-        s, c, size = where_is(i)
         slot = i % slots
-        return pltpu.make_async_copy(ref.at[first_seq + s, 0, pl.ds(pl.multiple_of(c * ITEM, ITEM), size)], buf.at[slot, pl.ds(0, size)], sem.at[slot])
+        size = pl.multiple_of((jnp.minimum(left[i], ITEM) + 15) // 16 * 16, 16)
+        return pltpu.make_async_copy(ref.at[first_seq + entry // 4, 0, pl.ds(pl.multiple_of(entry % 4 * ITEM, ITEM), size)], buf.at[slot, pl.ds(0, size)], sem.at[slot])
 
     def k_copy(i):
         return copy(i, key_ref, kbuf, k_sem)
@@ -214,106 +223,143 @@
     def v_copy(i):
         return copy(i, value_ref, vbuf, v_sem)
 
-    for i in range(slots - 1):
+    for i in range(slots - 2):
         @pl.when(i < total)
         def _():
             k_copy(i).start()
     for i in range(slots):
         vbuf[i] = jnp.zeros((ITEM, 256), BF16)
-        if i < slots - 1:
+        if i < slots - 2:
             @pl.when(i < total)
             def _():
                 v_copy(i).start()
 
-    for part in range(2):
-        qf[part] = q_ref[:, :, part * 128:(part + 1) * 128].reshape(768, 128).astype(F32)
-    knf[...] = kn_ref[...].astype(F32)
-    vnf[...] = vn_ref[...].astype(F32)
+    kn_out[...] = kn_ref[...]
+    vn_out[...] = vn_ref[...]
+    column = lax.broadcasted_iota(jnp.int32, (48, 768), 1)
+    row = lax.broadcasted_iota(jnp.int32, (48, 768), 0)
+    for n in range(16):
+        perm[n * 48:(n + 1) * 48] = jnp.where(column == row * 16 + n, 1.0, 0.0).astype(BF16)
+        back[n * 48:(n + 1) * 48] = jnp.where(column == row % 16 * 48 + row // 16 + 3 * n, 1.0, 0.0).astype(BF16)
+    qs[...] = jnp.dot(perm[...], q_ref[...].reshape(768, 256), preferred_element_type=F32).astype(BF16)
+    vnf[...] = vn_ref[pl.ds(pl.multiple_of(first_seq, 16), 16), :].astype(F32)
+    knf = kn_ref[pl.ds(pl.multiple_of(first_seq, 16), 16), :].astype(F32)
+    for n in range(16):
+        rows = slice(n * 48, (n + 1) * 48)
+        sn[rows] = jnp.broadcast_to(jnp.sum(qs[rows].astype(F32) * knf[n:n + 1], axis=1, keepdims=True), (48, 128))
     m_ref[...] = jnp.zeros_like(m_ref)
     l_ref[...] = jnp.ones_like(l_ref)
     acc[...] = jnp.zeros_like(acc)
 
-    def query(s):
-        return jnp.concatenate([qf[part, pl.ds(s, 48, stride=16), :] for part in range(2)], axis=1)
-
-    def scores(i):
-        s, _, _ = where_is(i)
-        q = query(s).astype(BF16)
-        sbuf[i % 2] = lax.dot_general(q, kbuf[i % slots], (((1,), (1,)), ((), ())), preferred_element_type=F32)
-
-    k_copy(0).wait()
-    scores(0)
-
-    @pl.loop(0, total)
-    def _(i):
-        @pl.when(i + slots - 1 < total)
-        def _():
-            k_copy(i + slots - 1).start()
-            v_copy(i + slots - 1).start()
-
-        after = jnp.minimum(i + 1, total - 1)
-
-        @pl.when(i + 1 < total)
-        def _():
-            k_copy(i + 1).wait()
-        v_copy(i).wait()
-
-        s_after, _, _ = where_is(after)
-        q_after = query(s_after).astype(BF16)
-        s_next = lax.dot_general(q_after, kbuf[after % slots], (((1,), (1,)), ((), ())), preferred_element_type=F32)
-
-        s, c, _ = where_is(i)
-        left = len_ref[first_seq + s] - c * ITEM
-        fresh = c == 0
-        q_now = query(s)
-        kn = knf[pl.ds(first_seq + s, 1), :]
-        vn = vnf[pl.ds(first_seq + s, 1), :]
-        score_new = jnp.sum(q_now * kn, axis=1, keepdims=True) * scale
-        m_old = jnp.where(fresh, score_new, m_ref[:, :1])
-        l_old = jnp.where(fresh, 1.0, l_ref[:, :1])
-        acc_old = jnp.where(fresh, jnp.broadcast_to(vn, acc.shape), acc[...])
-        x = sbuf[i % 2] * scale
-        x = jnp.where(lax.broadcasted_iota(jnp.int32, x.shape, 1) < left, x, -jnp.inf)
-        m_now = jnp.maximum(m_old, jnp.max(x, axis=1, keepdims=True))
-        alpha = jnp.exp(m_old - m_now)
-        p = jnp.exp(x - m_now)
-        l_now = l_old * alpha + jnp.sum(p, axis=1, keepdims=True)
-        acc_now = acc_old * alpha + jnp.dot(p.astype(BF16), vbuf[i % slots], preferred_element_type=F32)
-        m_ref[...] = jnp.broadcast_to(m_now, m_ref.shape)
-        l_ref[...] = jnp.broadcast_to(l_now, l_ref.shape)
-        acc[...] = acc_now
-        result = acc_now / l_now
-        for part in range(2):
-            of[part, pl.ds(pl.multiple_of(s * 48, 8), 48), :] = result[:, part * 128:(part + 1) * 128]
-        sbuf[(i + 1) % 2] = s_next
-
+    def rows_of(entry):
+        return pl.ds(pl.multiple_of(entry // 4 * 48, 16), 48)
+
+    def score(i):
+        return lax.dot_general(qs[rows_of(items[i]), :], kbuf[i % slots], (((1,), (1,)), ((), ())), preferred_element_type=F32)
+
+    lane = lax.broadcasted_iota(jnp.int32, (48, 128), 1)
+
+    halves = (slice(0, 128), slice(128, 256))
+    chunks = [slice(n * 128, (n + 1) * 128) for n in range(ITEM // 128)]
+
+    def pair_scores(pair, turn):
+        for n in range(2):
+            sbuf[turn, n] = score(2 * pair + n)
+
+    def weigh(pair, turn):
+        m, l = m_ref[...], l_ref[...]
+        for n in range(2):
+            i = 2 * pair + n
+            entry = items[i]
+            fresh = entry % 4 == 0
+            m_old = jnp.where(fresh, sn[rows_of(entry), :], m)
+            x = [jnp.where(lane < left[i] - c.start, sbuf[turn, n, :, c], -jnp.inf) for c in chunks]
+            top = functools.reduce(jnp.maximum, x)
+            m = jnp.maximum(m_old, jnp.broadcast_to(jnp.max(top, axis=1, keepdims=True), (48, 128)))
+            alpha = jnp.exp2((m_old - m) * power)
+            p = [jnp.exp2((v - m) * power) for v in x]
+            l = jnp.where(fresh, 1.0, l) * alpha + jnp.broadcast_to(jnp.sum(functools.reduce(jnp.add, p), axis=1, keepdims=True), (48, 128))
+            a_ref[turn, n] = alpha
+            r_ref[turn, n] = l
+            for c, v in zip(chunks, p):
+                pbuf[turn, n, :, c] = v.astype(BF16)
+        m_ref[...] = m
+        l_ref[...] = l
+
+    def blend(pair, turn):
+        for n in range(2):
+            i = 2 * pair + n
+            entry = items[i]
+            added = jnp.dot(pbuf[turn, n], vbuf[i % slots], preferred_element_type=F32)
+            alpha = a_ref[turn, n]
+            inverse = 1.0 / r_ref[turn, n]
+            fresh_row = vnf[pl.ds(entry // 4, 1), :]
+            for h in halves:
+                now = jnp.where(entry % 4 == 0, jnp.broadcast_to(fresh_row[:, h], (48, 128)), acc[:, h]) * alpha + added[:, h]
+                acc[:, h] = now
+                os[rows_of(entry), h] = (now * inverse).astype(BF16)
+
+    def arrive(copy, pair):
+        for n in range(2):
+            @pl.when(2 * pair + n < total)
+            def _():
+                copy(2 * pair + n).wait()
+
+    arrive(k_copy, 0)
+    pair_scores(0, 0)
+    weigh(0, 0)
+    arrive(k_copy, 1)
+    pair_scores(jnp.minimum(1, pairs - 1), 1)
+
+    @pl.loop(0, pairs)
+    def _(pair):
+        for n in range(2):
+            i = 2 * pair + slots - 2 + n
+
+            @pl.when(i < total)
+            def _():
+                k_copy(i).start()
+                v_copy(i).start()
+
+        arrive(k_copy, pair + 2)
+        arrive(v_copy, pair)
+        turn = pair % 2
+        blend(pair, turn)
+        weigh(jnp.minimum(pair + 1, pairs - 1), 1 - turn)
+        pair_scores(jnp.minimum(pair + 2, pairs - 1), turn)
+
+    mixed = jnp.dot(back[...], os[...], preferred_element_type=F32).astype(BF16)
     for h in range(48):
-        for part in range(2):
-            start = (h % 6) * 256 + part * 128
-            o_ref[h // 6, :, start:start + 128] = of[part, pl.ds(h, 16, stride=48), :].astype(BF16)
+        o_ref[h // 6, :, (h % 6) * 256:(h % 6 + 1) * 256] = mixed[h * 16:(h + 1) * 16]
 
 
 def attend(lengths, queries, key_new, value_new, key_cache, value_cache):
-    slots = 10
+    slots = 12
     vmem = pl.BlockSpec(memory_space=pltpu.VMEM)
-    hbm = pl.BlockSpec(memory_space=pl.ANY)
+    hbm = pl.BlockSpec(memory_space=pltpu.HBM)
     return pl.pallas_call(
         functools.partial(attend_kernel, slots),
-        out_shape=jax.ShapeDtypeStruct((8, 16, 1536), BF16),
+        out_shape=(jax.ShapeDtypeStruct((8, 16, 1536), BF16), jax.ShapeDtypeStruct((32, 256), BF16), jax.ShapeDtypeStruct((32, 256), BF16)),
         in_specs=[pl.BlockSpec(memory_space=pltpu.SMEM), vmem, vmem, vmem, hbm, hbm],
-        out_specs=vmem,
+        out_specs=(vmem, vmem, vmem),
         scratch_shapes=[
             pltpu.VMEM((slots, ITEM, 256), BF16),
             pltpu.VMEM((slots, ITEM, 256), BF16),
-            pltpu.VMEM((2, 768, 128), F32),
-            pltpu.VMEM((2, 768, 128), F32),
-            pltpu.VMEM((32, 256), F32),
-            pltpu.VMEM((32, 256), F32),
-            pltpu.VMEM((2, 48, ITEM), F32),
+            pltpu.VMEM((768, 768), BF16),
+            pltpu.VMEM((768, 768), BF16),
+            pltpu.VMEM((768, 256), BF16),
+            pltpu.VMEM((768, 256), BF16),
+            pltpu.VMEM((768, 128), F32),
+            pltpu.VMEM((16, 256), F32),
+            pltpu.VMEM((2, 2, 48, ITEM), F32),
+            pltpu.VMEM((2, 2, 48, ITEM), BF16),
             pltpu.VMEM((48, 256), F32),
             pltpu.VMEM((48, 128), F32),
             pltpu.VMEM((48, 128), F32),
-            pltpu.SMEM((64,), jnp.int32),
+            pltpu.VMEM((2, 2, 48, 128), F32),
+            pltpu.VMEM((2, 2, 48, 128), F32),
+            pltpu.SMEM((72,), jnp.int32),
+            pltpu.SMEM((72,), jnp.int32),
             pltpu.SemaphoreType.DMA((slots,)),
             pltpu.SemaphoreType.DMA((slots,)),
         ],
@@ -323,7 +369,7 @@
     )(lengths, queries, key_new, value_new, key_cache, value_cache)
 
 
-LAGS = (1, 4, 7, 10, 13)
+LAGS = (4, 9, 15, 22, 28)
 
 
 def mix_kernel(chunk, slots, o_ref, w_ref, x_ref, out_ref, o_all, wbuf, xrows, part, r0, r1, r2,
@@ -463,7 +509,7 @@
     chunk, slots = 512, 8
     chunks = width // chunk
     vmem = pl.BlockSpec(memory_space=pltpu.VMEM)
-    hbm = pl.BlockSpec(memory_space=pl.ANY)
+    hbm = pl.BlockSpec(memory_space=pltpu.HBM)
     sems = pltpu.SemaphoreType.DMA((chunks,))
     return pl.pallas_call(
         functools.partial(mix_kernel, chunk, slots),
@@ -483,16 +529,16 @@
             pltpu.SemaphoreType.DMA((8,)),
             pltpu.SemaphoreType.DMA((8,)),
         ] + [sems] * 12,
-        compiler_params=pltpu.CompilerParams(collective_id=1, has_side_effects=True, vmem_limit_bytes=56 * MIB),
+        compiler_params=pltpu.CompilerParams(collective_id=1, has_side_effects=True, vmem_limit_bytes=42 * MIB),
         cost_estimate=pl.CostEstimate(flops=2 * 128 * depth * width, bytes_accessed=depth * width * 2, transcendentals=0),
         name="mix",
-    )(attended, w_out, tokens)
+    )(attended, *(pltpu.with_memory_space_constraint(a, pltpu.HBM) for a in (w_out, tokens)))
 
 
 def solution(mesh):
     def local_step(tokens, w_query, w_key, w_value, w_out, key_cache, value_cache, lengths):
         queries, key_new, value_new = project_queries(tokens, w_query, w_key, w_value)
-        attended = attend(lengths, queries, key_new, value_new, key_cache, value_cache)
+        attended, key_new, value_new = attend(lengths, queries, key_new, value_new, key_cache, value_cache)
         out_tokens = mix(attended, w_out, tokens)
         return (out_tokens, key_new.reshape(32, 1, 256), value_new.reshape(32, 1, 256))
 

time: 149 us -> 129 us (0.87)
  Pallas kernels: 138 us -> 127 us
  local copies, waits for them, and re-layouts: 9.23 us -> 2.19 us
    unnamed x9 -> x3, local copies, waits for them, and re-layouts: 9.23 us -> 2.19 us
    pallas_call x1, Pallas kernels: 85.5 us -> 80 us  [mix(): pl.pallas_call(functools.partial(mix_kernel, chunk, slots), out_shape=jax...]
    pallas_call x1, Pallas kernels: 23.2 us -> 19 us  [attend(): pl.pallas_call(functools.partial(attend_kernel, slots), out_shape=(jax.Sh...]
    pallas_call x1, Pallas kernels: 29.5 us -> 27.8 us  [project_queries(): pl.pallas_call(functools.partial(query_kernel, groups, cols, depth, slots...]
where the time goes in v2:
time: 129 us; the launch traced here: 130 us
  Pallas kernels  127 us (98%)
  local copies, waits for them, and re-layouts  2.19 us (2%)
    pallas_call x1, Pallas kernels, mix(): pl.pallas_call(functools.partial(mix_kernel, chunk, slots), out_shape=jax...  80 us
    pallas_call x1, Pallas kernels, project_queries(): pl.pallas_call(functools.partial(query_kernel, groups, cols, depth, slots...  27.8 us
    pallas_call x1, Pallas kernels, attend(): pl.pallas_call(functools.partial(attend_kernel, slots), out_shape=(jax.Sh...  19 us

profile of v2, /device:TPU:0, one launch (start us, length us, event | category | flops | bytes accessed | tf_op | source)
XLA Modules:
  0.0 129.6 jit_solution(6444913651552836216)
XLA Ops:
  0.6 0.0 copy-start
  0.6 27.8 %query.1 = (bf16[48,16,256]{2,1,0:T(8,128)(2,1)S(1)}, bf16[32,256]{1,0:T(8,128)(2,1)S(1)}, bf16[32,256]{1,0:T(8,128)(2,1)S(1)}) custom-call(bf16[128,18432]{1,0:T(8,128)(2,1)} %x_ref.3, bf16[18432,1536]{1,0:T(8,128)(2,1)} %wq_ref.1, bf16[18432,256]{1,0:T(8,128)(2,1)} %wk_ref.1, bf16[18432,256]{1,0:T(8,128)(2,1)} %wv_ref.1), custom_call_target="tpu_custom_call" | custom-call | flops 7851737088 | bytes 61341696 | tf_op jit(solution)/shard_map/query/pallas_call | solution.py:162
  28.4 0.0 copy-done
  28.4 19.0 %attend.1 = (bf16[8,16,1536]{2,1,0:T(8,128)(2,1)S(1)}, bf16[32,256]{1,0:T(8,128)(2,1)}, bf16[32,256]{1,0:T(8,128)(2,1)}) custom-call(s32[32]{0:T(128)S(1)} %copy-done, bf16[48,16,256]{2,1,0:T(8,128)(2,1)S(1)} %get-tuple-element.9.q_ref, bf16[32,256]{1,0:T(8,128)(2,1)S(1)} %get-tuple-element.10.kn_ref, bf16[32,256]{1,0:T(8,128)(2,1)S(1)} %get-tuple-element.11.vn_ref, ...), custom_call_target="tpu_custom_call" | custom-call | flops 1610612736 | bytes 33554432 | tf_op jit(solution)/shard_map/attend/pallas_call | solution.py:340
  47.4 80.0 %mix.1 = bf16[128,18432]{1,0:T(8,128)(2,1)S(1)} custom-call(bf16[8,16,1536]{2,1,0:T(8,128)(2,1)S(1)} %get-tuple-element.12.o_ref, bf16[1536,18432]{1,0:T(8,128)(2,1)} %w_ref.1, bf16[128,18432]{1,0:T(8,128)(2,1)} %x_ref.3), custom_call_target="tpu_custom_call" | custom-call | flops 7247757312 | bytes 56623104 | tf_op jit(solution)/shard_map/mix/pallas_call | solution.py:514
  127.4 2.2 %copy.12 = bf16[128,18432]{1,0:T(8,128)(2,1)} copy(bf16[128,18432]{1,0:T(8,128)(2,1)S(1)} %mix.1) | data formatting | bytes 9437184
Async XLA Ops:
  0.6 27.8 %copy-start = (s32[32]{0:T(128)S(1)}, s32[32]{0:T(128)}, u32[]{:S(2)}) copy-start(s32[32]{0:T(128)} %len_ref.1) | copy-start | bytes 388

commit v3 on v2

--- a/solution.py
+++ b/solution.py
@@ -19,18 +19,17 @@
     return y, model, model // 2, model % 2
 
 
-def enter(others):
+def greet(others):
     y, model, _, _ = coordinates()
     me = y * 4 + model
     barrier = pltpu.get_barrier_semaphore()
     for offset in others:
         peer = (me + offset) % 8
         pl.semaphore_signal(barrier, inc=1, device_id={"heads": peer // 4, "model": peer % 4}, device_id_type=MESH)
-    pl.semaphore_wait(barrier, len(others))
-
-
-def query_kernel(groups, cols, depth, slots, kv_depth, x_ref, wq_ref, wk_ref, wv_ref, q_ref, kn_ref, vn_ref, xbuf, wbuf, kvbuf, acc, kvacc, qs, kvs, kv_all,
-                 x_sem, w_sem, kv_sem, q_send, q_recv, kv_send, kv_recv, self_sem):
+
+
+def query_kernel(groups, cols, depth, slots, kv_depth, x_ref, wq_ref, wk_ref, wv_ref, q_ref, kn_ref, vn_ref, perm, back, xbuf, wbuf, kvbuf, acc, kvacc, qs, kvs, kv_all,
+                 x_sem, w_sem, kv_sem, q_send, q_recv, kv_send, kv_recv, self_sem, kv_self_sem):
     y, model, _, _ = coordinates()
     me = y * 4 + model
     width = x_ref.shape[1]
@@ -55,7 +54,13 @@
         if i < slots:
             w_copy(i).start()
 
-    enter(range(1, 8))
+    greet(range(1, 8))
+    column = lax.broadcasted_iota(jnp.int32, (48, 768), 1)
+    row = lax.broadcasted_iota(jnp.int32, (48, 768), 0)
+    for n in range(16):
+        perm[n * 48:(n + 1) * 48] = jnp.where(column == row * 16 + n, 1.0, 0.0).astype(BF16)
+        back[n * 48:(n + 1) * 48] = jnp.where(column == row % 16 * 48 + row // 16 + 3 * n, 1.0, 0.0).astype(BF16)
+    pl.semaphore_wait(pltpu.get_barrier_semaphore(), 7)
 
     per_group = cols // 256
 
@@ -65,11 +70,11 @@
         rows = (peer % 4) * 2 + peer // 4
         return pltpu.make_async_remote_copy(
             src_ref=qs.at[head, pl.ds(rows * 16, 16)], dst_ref=q_ref.at[me * 6 + head],
-            send_sem=q_send.at[head * 8 + offset], recv_sem=q_recv.at[me * 6 + head],
+            send_sem=q_send, recv_sem=q_recv,
             device_id={"heads": peer // 4, "model": peer % 4}, device_id_type=MESH)
 
     def q_self(head):
-        return pltpu.make_async_copy(qs.at[head, pl.ds((model * 2 + y) * 16, 16)], q_ref.at[me * 6 + head], self_sem.at[1 + head])
+        return pltpu.make_async_copy(qs.at[head, pl.ds((model * 2 + y) * 16, 16)], q_ref.at[me * 6 + head], self_sem)
 
     @pl.loop(0, total)
     def _(i):
@@ -126,27 +131,23 @@
     def kv_send_copy(offset):
         peer = (model + offset) % 4
         return pltpu.make_async_remote_copy(
-            src_ref=kvs.at[pl.ds(peer * 32, 32)], dst_ref=kv_all.at[model], send_sem=kv_send.at[offset], recv_sem=kv_recv.at[model],
+            src_ref=kvs.at[pl.ds(peer * 32, 32)], dst_ref=kv_all.at[model], send_sem=kv_send, recv_sem=kv_recv,
             device_id={"heads": y, "model": peer}, device_id_type=MESH)
 
     for offset in (2, 3, 1):
         kv_send_copy(offset).start()
-    kv_self = pltpu.make_async_copy(kvs.at[pl.ds(model * 32, 32)], kv_all.at[model], self_sem.at[0])
+    kv_self = pltpu.make_async_copy(kvs.at[pl.ds(model * 32, 32)], kv_all.at[model], kv_self_sem)
     kv_self.start()
 
-    @pl.loop(0, 6)
-    def _(head):
-        q_self(head).wait()
-        for offset in range(1, 8):
-            q_copy(0, head, offset).wait_send()
-            src = (me + offset) % 8
-            pltpu.make_async_copy(q_ref.at[src * 6 + head], q_ref.at[src * 6 + head], q_recv.at[src * 6 + head]).wait()
-
+    def settle(ref, sem):
+        pltpu.make_async_copy(ref, ref, sem).wait()
+
+    settle(q_ref.at[pl.ds(0, 6)], self_sem)
+    settle(q_ref.at[pl.ds(0, 42)], q_send)
+    settle(q_ref.at[pl.ds(0, 42)], q_recv)
     kv_self.wait()
-    for offset in range(1, 4):
-        kv_send_copy(offset).wait_send()
-        src = (model + offset) % 4
-        pltpu.make_async_copy(kv_all.at[src], kv_all.at[src], kv_recv.at[src]).wait()
+    settle(kv_all.at[pl.ds(0, 3)], kv_send)
+    settle(kv_all.at[pl.ds(0, 3)], kv_recv)
     kn_ref[:, :128] = kv_all[0]
     kn_ref[:, 128:] = kv_all[1]
     vn_ref[:, :128] = kv_all[2]
@@ -161,9 +162,10 @@
     hbm = pl.BlockSpec(memory_space=pltpu.HBM)
     return pl.pallas_call(
         functools.partial(query_kernel, groups, cols, depth, slots, kv_depth),
-        out_shape=(jax.ShapeDtypeStruct((48, 16, 256), BF16), jax.ShapeDtypeStruct((32, 256), BF16), jax.ShapeDtypeStruct((32, 256), BF16)),
+        out_shape=(jax.ShapeDtypeStruct((48, 16, 256), BF16), jax.ShapeDtypeStruct((32, 256), BF16), jax.ShapeDtypeStruct((32, 256), BF16),
+                   jax.ShapeDtypeStruct((768, 768), BF16), jax.ShapeDtypeStruct((768, 768), BF16)),
         in_specs=[hbm, hbm, hbm, hbm],
-        out_specs=(vmem, vmem, vmem),
+        out_specs=(vmem,) * 5,
         scratch_shapes=[
             pltpu.VMEM((rows, width), BF16),
             pltpu.VMEM((slots, depth, cols), BF16),
@@ -176,12 +178,7 @@
             pltpu.SemaphoreType.DMA((width // depth,)),
             pltpu.SemaphoreType.DMA((slots,)),
             pltpu.SemaphoreType.DMA((width // kv_depth,)),
-            pltpu.SemaphoreType.DMA((48,)),
-            pltpu.SemaphoreType.DMA((48,)),
-            pltpu.SemaphoreType.DMA((4,)),
-            pltpu.SemaphoreType.DMA((4,)),
-            pltpu.SemaphoreType.DMA((7,)),
-        ],
+        ] + [pltpu.SemaphoreType.DMA] * 6,
         compiler_params=pltpu.CompilerParams(collective_id=0, has_side_effects=True, vmem_limit_bytes=48 * MIB),
         cost_estimate=pl.CostEstimate(flops=2 * rows * width * 1664, bytes_accessed=width * 1664 * 2, transcendentals=0),
         name="query",
@@ -191,7 +188,7 @@
 ITEM = 1024
 
 
-def attend_kernel(slots, len_ref, q_ref, kn_ref, vn_ref, key_ref, value_ref, o_ref, kn_out, vn_out, kbuf, vbuf, perm, back, qs, os, sn, vnf, sbuf, pbuf, acc, m_ref, l_ref, a_ref, r_ref, items, left, k_sem, v_sem):
+def attend_kernel(slots, len_ref, q_ref, kn_ref, vn_ref, perm, back, key_ref, value_ref, o_ref, kn_out, vn_out, kbuf, vbuf, qs, os, sn, vnf, sbuf, pbuf, acc, m_ref, l_ref, a_ref, r_ref, items, left, k_sem, v_sem):
     y = lax.axis_index("heads")
     first_seq = y * 16
     power = 256 ** -0.5 * 1.4426950408889634
@@ -211,36 +208,26 @@
     left[total] = 0
     pairs = (total + 1) // 2
 
-    def copy(i, ref, buf, sem):
+    def copy(i, ref, buf, sem, whole=False):
         entry = items[i]
         slot = i % slots
-        size = pl.multiple_of((jnp.minimum(left[i], ITEM) + 15) // 16 * 16, 16)
+        size = pl.multiple_of((jnp.where(whole, ITEM, jnp.minimum(left[i], ITEM)) + 15) // 16 * 16, 16)
         return pltpu.make_async_copy(ref.at[first_seq + entry // 4, 0, pl.ds(pl.multiple_of(entry % 4 * ITEM, ITEM), size)], buf.at[slot, pl.ds(0, size)], sem.at[slot])
 
     def k_copy(i):
         return copy(i, key_ref, kbuf, k_sem)
 
     def v_copy(i):
-        return copy(i, value_ref, vbuf, v_sem)
+        return copy(i, value_ref, vbuf, v_sem, i < slots)
 
     for i in range(slots - 2):
         @pl.when(i < total)
         def _():
             k_copy(i).start()
-    for i in range(slots):
-        vbuf[i] = jnp.zeros((ITEM, 256), BF16)
-        if i < slots - 2:
-            @pl.when(i < total)
-            def _():
-                v_copy(i).start()
+            v_copy(i).start()
 
     kn_out[...] = kn_ref[...]
     vn_out[...] = vn_ref[...]
-    column = lax.broadcasted_iota(jnp.int32, (48, 768), 1)
-    row = lax.broadcasted_iota(jnp.int32, (48, 768), 0)
-    for n in range(16):
-        perm[n * 48:(n + 1) * 48] = jnp.where(column == row * 16 + n, 1.0, 0.0).astype(BF16)
-        back[n * 48:(n + 1) * 48] = jnp.where(column == row % 16 * 48 + row // 16 + 3 * n, 1.0, 0.0).astype(BF16)
     qs[...] = jnp.dot(perm[...], q_ref[...].reshape(768, 256), preferred_element_type=F32).astype(BF16)
     vnf[...] = vn_ref[pl.ds(pl.multiple_of(first_seq, 16), 16), :].astype(F32)
     knf = kn_ref[pl.ds(pl.multiple_of(first_seq, 16), 16), :].astype(F32)
@@ -333,20 +320,18 @@
         o_ref[h // 6, :, (h % 6) * 256:(h % 6 + 1) * 256] = mixed[h * 16:(h + 1) * 16]
 
 
-def attend(lengths, queries, key_new, value_new, key_cache, value_cache):
+def attend(lengths, queries, key_new, value_new, perm, back, key_cache, value_cache):
     slots = 12
     vmem = pl.BlockSpec(memory_space=pltpu.VMEM)
     hbm = pl.BlockSpec(memory_space=pltpu.HBM)
     return pl.pallas_call(
         functools.partial(attend_kernel, slots),
         out_shape=(jax.ShapeDtypeStruct((8, 16, 1536), BF16), jax.ShapeDtypeStruct((32, 256), BF16), jax.ShapeDtypeStruct((32, 256), BF16)),
-        in_specs=[pl.BlockSpec(memory_space=pltpu.SMEM), vmem, vmem, vmem, hbm, hbm],
+        in_specs=[pl.BlockSpec(memory_space=pltpu.SMEM), vmem, vmem, vmem, vmem, vmem, hbm, hbm],
         out_specs=(vmem, vmem, vmem),
         scratch_shapes=[
             pltpu.VMEM((slots, ITEM, 256), BF16),
             pltpu.VMEM((slots, ITEM, 256), BF16),
-            pltpu.VMEM((768, 768), BF16),
-            pltpu.VMEM((768, 768), BF16),
             pltpu.VMEM((768, 256), BF16),
             pltpu.VMEM((768, 256), BF16),
             pltpu.VMEM((768, 128), F32),
@@ -366,14 +351,14 @@
         compiler_params=pltpu.CompilerParams(vmem_limit_bytes=40 * MIB),
         cost_estimate=pl.CostEstimate(flops=4 * 16 * 48 * 2048 * 256, bytes_accessed=16 * 2048 * 1024, transcendentals=16 * 48 * 2048),
         name="attend",
-    )(lengths, queries, key_new, value_new, key_cache, value_cache)
-
-
-LAGS = (4, 9, 15, 22, 28)
+    )(lengths, queries, key_new, value_new, perm, back, key_cache, value_cache)
+
+
+LAGS = (2, 5, 9, 12, 15)
 
 
 def mix_kernel(chunk, slots, o_ref, w_ref, x_ref, out_ref, o_all, wbuf, xrows, part, r0, r1, r2,
-               w_sem, x_sem, o_send, o_recv, s0s, s0r, s1s, s1r, s2s, s2r, g1s, g1r, g2s, g2r, g3s, g3r):
+               w_sem, x_sem, o_send, o_recv, o_self_sem, s0s, s1s, s2s, g1s, g2s, g3s, g3r, s0r, s1r, s2r, g1r, g2r):
     y, model, x, core = coordinates()
     me = y * 4 + model
     width = w_ref.shape[1]
@@ -393,25 +378,23 @@
     x_copy = pltpu.make_async_copy(x_ref.at[pl.ds(own * 16, 16)], xrows, x_sem)
     x_copy.start()
 
-    enter(range(1, 8))
+    greet(range(1, 8))
+    pl.semaphore_wait(pltpu.get_barrier_semaphore(), 7)
 
     mine = model * 2 + y
 
     def o_copy(offset):
         peer = (me + offset) % 8
         return pltpu.make_async_remote_copy(
-            src_ref=o_ref.at[peer], dst_ref=o_all.at[pl.ds(mine * 16, 16)], send_sem=o_send.at[offset], recv_sem=o_recv.at[me],
+            src_ref=o_ref.at[peer], dst_ref=o_all.at[pl.ds(mine * 16, 16)], send_sem=o_send, recv_sem=o_recv,
             device_id={"heads": peer // 4, "model": peer % 4}, device_id_type=MESH)
 
     for offset in range(1, 8):
         o_copy(offset).start()
-    o_self = pltpu.make_async_copy(o_ref.at[me], o_all.at[pl.ds(mine * 16, 16)], o_send.at[0])
+    o_self = pltpu.make_async_copy(o_ref.at[me], o_all.at[pl.ds(mine * 16, 16)], o_self_sem)
     o_self.start()
     o_self.wait()
-    for offset in range(1, 8):
-        src = (me + offset) % 8
-        block = o_all.at[pl.ds(((src % 4) * 2 + src // 4) * 16, 16)]
-        pltpu.make_async_copy(block, block, o_recv.at[src]).wait()
+    pltpu.make_async_copy(o_all.at[pl.ds(0, 112)], o_all.at[pl.ds(0, 112)], o_recv).wait()
     x_copy.wait()
 
     def remote(src, dst, send, recv, device):
@@ -422,25 +405,25 @@
     cols = lambda j: pl.ds(pl.multiple_of(j * chunk, chunk), chunk)
 
     def s0(j):
-        return remote(part.at[j, pl.ds((1 - core) * 64, 64)], r0.at[j], s0s.at[j], s0r.at[j], partner)
+        return remote(part.at[j, pl.ds((1 - core) * 64, 64)], r0.at[j], s0s, s0r.at[j], partner)
 
     def s1(j):
-        return remote(part.at[j, pl.ds(half + (1 - first) * 32, 32)], r1.at[j], s1s.at[j], s1r.at[j], along_first)
+        return remote(part.at[j, pl.ds(half + (1 - first) * 32, 32)], r1.at[j], s1s, s1r.at[j], along_first)
 
     def s2(j):
-        return remote(part.at[j, pl.ds(quarter + (1 - second) * 16, 16)], r2.at[j], s2s.at[j], s2r.at[j], along_second)
+        return remote(part.at[j, pl.ds(quarter + (1 - second) * 16, 16)], r2.at[j], s2s, s2r.at[j], along_second)
 
     def g1(j):
         piece = out_ref.at[pl.ds(eighth, 16), cols(j)]
-        return remote(piece, piece, g1s.at[j], g1r.at[j], along_second)
+        return remote(piece, piece, g1s, g1r.at[j], along_second)
 
     def g2(j):
         piece = out_ref.at[pl.ds(quarter, 32), cols(j)]
-        return remote(piece, piece, g2s.at[j], g2r.at[j], along_first)
+        return remote(piece, piece, g2s, g2r.at[j], along_first)
 
     def g3(j):
         piece = out_ref.at[pl.ds(half, 64), cols(j)]
-        return remote(piece, piece, g3s.at[j], g3r.at[j], partner)
+        return remote(piece, piece, g3s, g3r, partner)
 
     def arrived(ref, sem):
         pltpu.make_async_copy(ref, ref, sem).wait()
@@ -494,19 +477,15 @@
         at(t, LAGS[3], stage4)
         at(t, LAGS[4], stage5)
 
-    for offset in range(1, 8):
-        o_copy(offset).wait_send()
-
-    @pl.loop(0, chunks)
-    def _(j):
-        arrived(out_ref.at[pl.ds((1 - core) * 64, 64), cols(j)], g3r.at[j])
-        for copy in (s0, s1, s2, g1, g2, g3):
-            copy(j).wait_send()
+    arrived(o_ref.at[pl.ds(0, 7)], o_send)
+    arrived(out_ref.at[pl.ds(0, 64)], g3r)
+    for ref, sem in ((r0, s0s), (r1, s1s), (r2, s2s), (out_ref.at[pl.ds(0, 16)], g1s), (out_ref.at[pl.ds(0, 32)], g2s), (out_ref.at[pl.ds(0, 64)], g3s)):
+        arrived(ref, sem)
 
 
 def mix(attended, w_out, tokens):
     depth, width = w_out.shape
-    chunk, slots = 512, 8
+    chunk, slots = 1024, 4
     chunks = width // chunk
     vmem = pl.BlockSpec(memory_space=pltpu.VMEM)
     hbm = pl.BlockSpec(memory_space=pltpu.HBM)
@@ -525,10 +504,7 @@
             pltpu.VMEM((chunks, 32, chunk), F32),
             pltpu.VMEM((chunks, 16, chunk), F32),
             pltpu.SemaphoreType.DMA((slots,)),
-            pltpu.SemaphoreType.DMA,
-            pltpu.SemaphoreType.DMA((8,)),
-            pltpu.SemaphoreType.DMA((8,)),
-        ] + [sems] * 12,
+        ] + [pltpu.SemaphoreType.DMA] * 11 + [sems] * 5,
         compiler_params=pltpu.CompilerParams(collective_id=1, has_side_effects=True, vmem_limit_bytes=42 * MIB),
         cost_estimate=pl.CostEstimate(flops=2 * 128 * depth * width, bytes_accessed=depth * width * 2, transcendentals=0),
         name="mix",
@@ -537,8 +513,8 @@
 
 def solution(mesh):
     def local_step(tokens, w_query, w_key, w_value, w_out, key_cache, value_cache, lengths):
-        queries, key_new, value_new = project_queries(tokens, w_query, w_key, w_value)
-        attended, key_new, value_new = attend(lengths, queries, key_new, value_new, key_cache, value_cache)
+        queries, key_new, value_new, perm, back = project_queries(tokens, w_query, w_key, w_value)
+        attended, key_new, value_new = attend(lengths, queries, key_new, value_new, perm, back, key_cache, value_cache)
         out_tokens = mix(attended, w_out, tokens)
         return (out_tokens, key_new.reshape(32, 1, 256), value_new.reshape(32, 1, 256))
 

time: 129 us -> 125 us (0.969); the launches traced: 130 us -> 123 us
  Pallas kernels: 127 us -> 120 us
    pallas_call x1, Pallas kernels: 80 us -> 72.2 us  [mix(): pl.pallas_call(functools.partial(mix_kernel, chunk, slots), out_shape=jax...]
    pallas_call x1, Pallas kernels: 19 us -> 21.4 us  [attend(): pl.pallas_call(functools.partial(attend_kernel, slots), out_shape=(jax.Sh...]
where the time goes in v3:
time: 125 us; the launch traced here: 123 us
  Pallas kernels  120 us (96%)
  local copies, waits for them, and re-layouts  2.19 us (2%)
    pallas_call x1, Pallas kernels, mix(): pl.pallas_call(functools.partial(mix_kernel, chunk, slots), out_shape=jax...  72.2 us
    pallas_call x1, Pallas kernels, project_queries(): pl.pallas_call(functools.partial(query_kernel, groups, cols, depth, slots...  26.8 us
    pallas_call x1, Pallas kernels, attend(): pl.pallas_call(functools.partial(attend_kernel, slots), out_shape=(jax.Sh...  21.4 us

profile of v3, /device:TPU:0, one launch (start us, length us, event | category | flops | bytes accessed | tf_op | source)
XLA Modules:
  0.0 123.3 jit_solution(1784330717025907076)
XLA Ops:
  0.6 0.0 copy-start
  0.6 26.8 %query.1 = (bf16[48,16,256]{2,1,0:T(8,128)(2,1)S(1)}, bf16[32,256]{1,0:T(8,128)(2,1)S(1)}, bf16[32,256]{1,0:T(8,128)(2,1)S(1)}, bf16[768,768]{1,0:T(8,128)(2,1)S(1)}, bf16[768,768]{1,0:T(8,128)(2,1)S(1)}) custom-call(bf16[128,18432]{1,0:T(8,128)(2,1)} %x_ref.3, bf16[18432,1536]{1,0:T(8,128)(2,1)} %wq_ref.1, bf16[18432,256]{1,0:T(8,128)(2,1)} %wk_ref.1, ...), custom_call_target="tpu_custom_call" | custom-call | flops 7851737088 | bytes 61341696 | tf_op jit(solution)/shard_map/query/pallas_call | solution.py:163
  27.4 0.0 copy-done
  27.5 21.4 %attend.1 = (bf16[8,16,1536]{2,1,0:T(8,128)(2,1)S(1)}, bf16[32,256]{1,0:T(8,128)(2,1)}, bf16[32,256]{1,0:T(8,128)(2,1)}) custom-call(s32[32]{0:T(128)S(1)} %copy-done, bf16[48,16,256]{2,1,0:T(8,128)(2,1)S(1)} %get-tuple-element.11.q_ref, bf16[32,256]{1,0:T(8,128)(2,1)S(1)} %get-tuple-element.12.kn_ref, bf16[32,256]{1,0:T(8,128)(2,1)S(1)} %get-tuple-element.13.vn_ref, ...), custom_call_target="tpu_custom_call" | custom-call | flops 1610612736 | bytes 33554432 | tf_op jit(solution)/shard_map/attend/pallas_call | solution.py:327
  48.8 72.2 %mix.1 = bf16[128,18432]{1,0:T(8,128)(2,1)S(1)} custom-call(bf16[8,16,1536]{2,1,0:T(8,128)(2,1)S(1)} %get-tuple-element.16.o_ref, bf16[1536,18432]{1,0:T(8,128)(2,1)} %w_ref.1, bf16[128,18432]{1,0:T(8,128)(2,1)} %x_ref.3), custom_call_target="tpu_custom_call" | custom-call | flops 7247757312 | bytes 56623104 | tf_op jit(solution)/shard_map/mix/pallas_call | solution.py:493
  121.1 2.2 %copy.12 = bf16[128,18432]{1,0:T(8,128)(2,1)} copy(bf16[128,18432]{1,0:T(8,128)(2,1)S(1)} %mix.1) | data formatting | bytes 9437184
Async XLA Ops:
  0.6 26.8 %copy-start = (s32[32]{0:T(128)S(1)}, s32[32]{0:T(128)}, u32[]{:S(2)}) copy-start(s32[32]{0:T(128)} %len_ref.1) | copy-start | bytes 388

commit v4 on v3

--- a/solution.py
+++ b/solution.py
@@ -188,31 +188,32 @@
 ITEM = 1024
 
 
-def attend_kernel(slots, len_ref, q_ref, kn_ref, vn_ref, perm, back, key_ref, value_ref, o_ref, kn_out, vn_out, kbuf, vbuf, qs, os, sn, vnf, sbuf, pbuf, acc, m_ref, l_ref, a_ref, r_ref, items, left, k_sem, v_sem):
+def attend_kernel(slots, len_ref, q_ref, kn_ref, vn_ref, perm, back, key_ref, value_ref, o_ref, kn_out, vn_out, kbuf, vbuf, qs, os, sn, vnf, sbuf, pbuf, acc, m_ref, l_ref, a_ref, r_ref, items, left, sizes, k_sem, v_sem):
     y = lax.axis_index("heads")
     first_seq = y * 16
     power = 256 ** -0.5 * 1.4426950408889634
 
     def list_seq(s, count):
         length = len_ref[first_seq + s]
-        chunks = (length + ITEM - 1) // ITEM
+        chunks = (length + ITEM - 1) >> 10
         for c in range(4):
             @pl.when(c < chunks)
             def _():
                 items[count + c] = s * 4 + c
                 left[count + c] = length - c * ITEM
+                sizes[count + c] = jnp.minimum((length - c * ITEM + 15) & ~15, ITEM)
         return count + chunks
 
     total = lax.fori_loop(0, 16, list_seq, jnp.int32(0))
-    items[total] = items[total - 1] // 4 * 4 + 3
+    items[total] = items[total - 1] | 3
     left[total] = 0
-    pairs = (total + 1) // 2
+    pairs = (total + 1) >> 1
 
     def copy(i, ref, buf, sem, whole=False):
         entry = items[i]
-        slot = i % slots
-        size = pl.multiple_of((jnp.where(whole, ITEM, jnp.minimum(left[i], ITEM)) + 15) // 16 * 16, 16)
-        return pltpu.make_async_copy(ref.at[first_seq + entry // 4, 0, pl.ds(pl.multiple_of(entry % 4 * ITEM, ITEM), size)], buf.at[slot, pl.ds(0, size)], sem.at[slot])
+        slot = i & (slots - 1)
+        size = pl.multiple_of(jnp.where(whole, ITEM, sizes[i]), 16)
+        return pltpu.make_async_copy(ref.at[first_seq + (entry >> 2), 0, pl.ds(pl.multiple_of((entry & 3) * ITEM, ITEM), size)], buf.at[slot, pl.ds(0, size)], sem.at[slot])
 
     def k_copy(i):
         return copy(i, key_ref, kbuf, k_sem)
@@ -239,10 +240,10 @@
     acc[...] = jnp.zeros_like(acc)
 
     def rows_of(entry):
-        return pl.ds(pl.multiple_of(entry // 4 * 48, 16), 48)
+        return pl.ds(pl.multiple_of((entry >> 2) * 48, 16), 48)
 
     def score(i):
-        return lax.dot_general(qs[rows_of(items[i]), :], kbuf[i % slots], (((1,), (1,)), ((), ())), preferred_element_type=F32)
+        return lax.dot_general(qs[rows_of(items[i]), :], kbuf[i & (slots - 1)], (((1,), (1,)), ((), ())), preferred_element_type=F32)
 
     lane = lax.broadcasted_iota(jnp.int32, (48, 128), 1)
 
@@ -258,7 +259,7 @@
         for n in range(2):
             i = 2 * pair + n
             entry = items[i]
-            fresh = entry % 4 == 0
+            fresh = (entry & 3) == 0
             m_old = jnp.where(fresh, sn[rows_of(entry), :], m)
             x = [jnp.where(lane < left[i] - c.start, sbuf[turn, n, :, c], -jnp.inf) for c in chunks]
             top = functools.reduce(jnp.maximum, x)
@@ -277,12 +278,12 @@
         for n in range(2):
             i = 2 * pair + n
             entry = items[i]
-            added = jnp.dot(pbuf[turn, n], vbuf[i % slots], preferred_element_type=F32)
+            added = jnp.dot(pbuf[turn, n], vbuf[i & (slots - 1)], preferred_element_type=F32)
             alpha = a_ref[turn, n]
             inverse = 1.0 / r_ref[turn, n]
-            fresh_row = vnf[pl.ds(entry // 4, 1), :]
+            fresh_row = vnf[pl.ds((entry >> 2), 1), :]
             for h in halves:
-                now = jnp.where(entry % 4 == 0, jnp.broadcast_to(fresh_row[:, h], (48, 128)), acc[:, h]) * alpha + added[:, h]
+                now = jnp.where((entry & 3) == 0, jnp.broadcast_to(fresh_row[:, h], (48, 128)), acc[:, h]) * alpha + added[:, h]
                 acc[:, h] = now
                 os[rows_of(entry), h] = (now * inverse).astype(BF16)
 
@@ -310,7 +311,7 @@
 
         arrive(k_copy, pair + 2)
         arrive(v_copy, pair)
-        turn = pair % 2
+        turn = pair & 1
         blend(pair, turn)
         weigh(jnp.minimum(pair + 1, pairs - 1), 1 - turn)
         pair_scores(jnp.minimum(pair + 2, pairs - 1), turn)
@@ -321,7 +322,7 @@
 
 
 def attend(lengths, queries, key_new, value_new, perm, back, key_cache, value_cache):
-    slots = 12
+    slots = 16
     vmem = pl.BlockSpec(memory_space=pltpu.VMEM)
     hbm = pl.BlockSpec(memory_space=pltpu.HBM)
     return pl.pallas_call(
@@ -345,6 +346,7 @@
             pltpu.VMEM((2, 2, 48, 128), F32),
             pltpu.SMEM((72,), jnp.int32),
             pltpu.SMEM((72,), jnp.int32),
+            pltpu.SMEM((72,), jnp.int32),
             pltpu.SemaphoreType.DMA((slots,)),
             pltpu.SemaphoreType.DMA((slots,)),
         ],
@@ -354,7 +356,7 @@
     )(lengths, queries, key_new, value_new, perm, back, key_cache, value_cache)
 
 
-LAGS = (2, 5, 9, 12, 15)
+LAGS = (2, 5, 10, 14, 17)
 
 
 def mix_kernel(chunk, slots, o_ref, w_ref, x_ref, out_ref, o_all, wbuf, xrows, part, r0, r1, r2,

time: 125 us -> 121 us (0.968); the launches traced: 123 us -> 121 us
  Pallas kernels: 120 us -> 118 us
    pallas_call x1, Pallas kernels: 21.4 us -> 17.9 us  [attend(): pl.pallas_call(functools.partial(attend_kernel, slots), out_shape=(jax.Sh...]
where the time goes in v4:
time: 121 us
  Pallas kernels  118 us (98%)
  local copies, waits for them, and re-layouts  2.19 us (2%)
    pallas_call x1, Pallas kernels, mix(): pl.pallas_call(functools.partial(mix_kernel, chunk, slots), out_shape=jax...  73.5 us
    pallas_call x1, Pallas kernels, project_queries(): pl.pallas_call(functools.partial(query_kernel, groups, cols, depth, slots...  26.8 us
    pallas_call x1, Pallas kernels, attend(): pl.pallas_call(functools.partial(attend_kernel, slots), out_shape=(jax.Sh...  17.9 us

profile of v4, /device:TPU:0, one launch (start us, length us, event | category | flops | bytes accessed | tf_op | source)
XLA Modules:
  0.0 121.0 jit_solution(3899199062361396823)
XLA Ops:
  0.6 0.0 copy-start
  0.6 26.8 %query.1 = (bf16[48,16,256]{2,1,0:T(8,128)(2,1)S(1)}, bf16[32,256]{1,0:T(8,128)(2,1)S(1)}, bf16[32,256]{1,0:T(8,128)(2,1)S(1)}, bf16[768,768]{1,0:T(8,128)(2,1)S(1)}, bf16[768,768]{1,0:T(8,128)(2,1)S(1)}) custom-call(bf16[128,18432]{1,0:T(8,128)(2,1)} %x_ref.3, bf16[18432,1536]{1,0:T(8,128)(2,1)} %wq_ref.1, bf16[18432,256]{1,0:T(8,128)(2,1)} %wk_ref.1, ...), custom_call_target="tpu_custom_call" | custom-call | flops 7851737088 | bytes 61341696 | tf_op jit(solution)/shard_map/query/pallas_call | solution.py:163
  27.4 0.0 copy-done
  27.5 17.9 %attend.1 = (bf16[8,16,1536]{2,1,0:T(8,128)(2,1)S(1)}, bf16[32,256]{1,0:T(8,128)(2,1)}, bf16[32,256]{1,0:T(8,128)(2,1)}) custom-call(s32[32]{0:T(128)S(1)} %copy-done, bf16[48,16,256]{2,1,0:T(8,128)(2,1)S(1)} %get-tuple-element.11.q_ref, bf16[32,256]{1,0:T(8,128)(2,1)S(1)} %get-tuple-element.12.kn_ref, bf16[32,256]{1,0:T(8,128)(2,1)S(1)} %get-tuple-element.13.vn_ref, ...), custom_call_target="tpu_custom_call" | custom-call | flops 1610612736 | bytes 33554432 | tf_op jit(solution)/shard_map/attend/pallas_call | solution.py:328
  45.4 73.5 %mix.1 = bf16[128,18432]{1,0:T(8,128)(2,1)S(1)} custom-call(bf16[8,16,1536]{2,1,0:T(8,128)(2,1)S(1)} %get-tuple-element.16.o_ref, bf16[1536,18432]{1,0:T(8,128)(2,1)} %w_ref.1, bf16[128,18432]{1,0:T(8,128)(2,1)} %x_ref.3), custom_call_target="tpu_custom_call" | custom-call | flops 7247757312 | bytes 56623104 | tf_op jit(solution)/shard_map/mix/pallas_call | solution.py:495
  118.8 2.2 %copy.12 = bf16[128,18432]{1,0:T(8,128)(2,1)} copy(bf16[128,18432]{1,0:T(8,128)(2,1)S(1)} %mix.1) | data formatting | bytes 9437184
Async XLA Ops:
  0.6 26.8 %copy-start = (s32[32]{0:T(128)S(1)}, s32[32]{0:T(128)}, u32[]{:S(2)}) copy-start(s32[32]{0:T(128)} %len_ref.1) | copy-start | bytes 388

commit v5 on v4

--- a/solution.py
+++ b/solution.py
@@ -267,7 +267,7 @@
             alpha = jnp.exp2((m_old - m) * power)
             p = [jnp.exp2((v - m) * power) for v in x]
             l = jnp.where(fresh, 1.0, l) * alpha + jnp.broadcast_to(jnp.sum(functools.reduce(jnp.add, p), axis=1, keepdims=True), (48, 128))
-            a_ref[turn, n] = alpha
+            a_ref[turn, n] = jnp.where(fresh, alpha.astype(BF16).astype(F32), alpha)
             r_ref[turn, n] = l
             for c, v in zip(chunks, p):
                 pbuf[turn, n, :, c] = v.astype(BF16)

time: 121 us -> 121 us (level)
    pallas_call x1, Pallas kernels: 17.9 us -> 20 us  [attend(): pl.pallas_call(functools.partial(attend_kernel, slots), out_shape=(jax.Sh...]
    pallas_call x1, Pallas kernels: 73.5 us -> 71.7 us  [mix(): pl.pallas_call(functools.partial(mix_kernel, chunk, slots), out_shape=jax...]
where the time goes in v5:
time: 121 us
  Pallas kernels  118 us (98%)
  local copies, waits for them, and re-layouts  2.19 us (2%)
    pallas_call x1, Pallas kernels, mix(): pl.pallas_call(functools.partial(mix_kernel, chunk, slots), out_shape=jax...  71.7 us
    pallas_call x1, Pallas kernels, project_queries(): pl.pallas_call(functools.partial(query_kernel, groups, cols, depth, slots...  26.8 us
    pallas_call x1, Pallas kernels, attend(): pl.pallas_call(functools.partial(attend_kernel, slots), out_shape=(jax.Sh...  20 us

profile of v5, /device:TPU:0, one launch (start us, length us, event | category | flops | bytes accessed | tf_op | source)
XLA Modules:
  0.0 121.3 jit_solution(5974424714073232343)
XLA Ops:
  0.6 0.0 copy-start
  0.6 26.8 %query.1 = (bf16[48,16,256]{2,1,0:T(8,128)(2,1)S(1)}, bf16[32,256]{1,0:T(8,128)(2,1)S(1)}, bf16[32,256]{1,0:T(8,128)(2,1)S(1)}, bf16[768,768]{1,0:T(8,128)(2,1)S(1)}, bf16[768,768]{1,0:T(8,128)(2,1)S(1)}) custom-call(bf16[128,18432]{1,0:T(8,128)(2,1)} %x_ref.3, bf16[18432,1536]{1,0:T(8,128)(2,1)} %wq_ref.1, bf16[18432,256]{1,0:T(8,128)(2,1)} %wk_ref.1, ...), custom_call_target="tpu_custom_call" | custom-call | flops 7851737088 | bytes 61341696 | tf_op jit(solution)/shard_map/query/pallas_call | solution.py:163
  27.4 0.0 copy-done
  27.5 20.0 %attend.1 = (bf16[8,16,1536]{2,1,0:T(8,128)(2,1)S(1)}, bf16[32,256]{1,0:T(8,128)(2,1)}, bf16[32,256]{1,0:T(8,128)(2,1)}) custom-call(s32[32]{0:T(128)S(1)} %copy-done, bf16[48,16,256]{2,1,0:T(8,128)(2,1)S(1)} %get-tuple-element.11.q_ref, bf16[32,256]{1,0:T(8,128)(2,1)S(1)} %get-tuple-element.12.kn_ref, bf16[32,256]{1,0:T(8,128)(2,1)S(1)} %get-tuple-element.13.vn_ref, ...), custom_call_target="tpu_custom_call" | custom-call | flops 1610612736 | bytes 33554432 | tf_op jit(solution)/shard_map/attend/pallas_call | solution.py:328
  47.4 71.7 %mix.1 = bf16[128,18432]{1,0:T(8,128)(2,1)S(1)} custom-call(bf16[8,16,1536]{2,1,0:T(8,128)(2,1)S(1)} %get-tuple-element.16.o_ref, bf16[1536,18432]{1,0:T(8,128)(2,1)} %w_ref.1, bf16[128,18432]{1,0:T(8,128)(2,1)} %x_ref.3), custom_call_target="tpu_custom_call" | custom-call | flops 7247757312 | bytes 56623104 | tf_op jit(solution)/shard_map/mix/pallas_call | solution.py:495
  119.2 2.2 %copy.12 = bf16[128,18432]{1,0:T(8,128)(2,1)} copy(bf16[128,18432]{1,0:T(8,128)(2,1)S(1)} %mix.1) | data formatting | bytes 9437184
Async XLA Ops:
  0.6 26.8 %copy-start = (s32[32]{0:T(128)S(1)}, s32[32]{0:T(128)}, u32[]{:S(2)}) copy-start(s32[32]{0:T(128)} %len_ref.1) | copy-start | bytes 388
